TPU v7x, 256 devices: a whole 4x4x8 slice. The times are simulated.
256 devices in a mesh: ep: 128 (over x, z, y), dp: 2 (over core).
Axes of the slice: x: 4, y: 4, z: 8, core: 2. Of those that a mesh axis runs over, the one named last changes fastest.
Arguments:
- tokens: bfloat16 [32768, 768], P(('ep', 'dp')), may hold values from -6 to 6
- routing: int32 [32768, 1], P(('ep', 'dp')), may hold values from 0 to 127; in each aligned block of 128 rows (0 to 127, 128 to 255, ...) at most 2 rows name the same one
- gate_prob: float32 [32768], P(('ep', 'dp')), may hold values from 0.2 to 1
- up_weight: bfloat16 [128, 768, 3072], P('ep', None, 'dp'), may hold values from -0.21875 to 0.21875
- down_weight: bfloat16 [128, 3072, 768], P('ep', 'dp'), may hold values from -0.109375 to 0.109375
- out_grad: bfloat16 [32768, 768], P(('ep', 'dp')), may hold values from -1.5 to 1.5
Outputs:
- output: bfloat16 [32768, 768], P(('ep', 'dp'))
- token_grad: bfloat16 [32768, 768], P(('ep', 'dp'))
- prob_grad: float32 [32768], P(('ep', 'dp'))
- up_grad: bfloat16 [128, 768, 3072], P('ep', None, 'dp')
- down_grad: bfloat16 [128, 3072, 768], P('ep', 'dp')
Inputs may be any that keep to these rules, and one draw needn't show every extreme that they name: `routing`: among the 128 rows of one device (devices in the order of ep, then dp) no expert is named more than 2 times; in some devices' rows some expert is named exactly 2 times; every expert is named somewhere.
All inputs are finite; a program needn't handle non-finite values.
Results may differ from a plain program's by a relative error of at most 0.0058.
Values may be sent and summed in bfloat16 or wider, within the bound.
No kernel may reach another device: no remote copies, remote signals or barrier semaphores. Data moves between devices by JAX's collectives and lax.ppermute only.
A program may use at most 64 MiB of HBM per device.

v0:
```python
import jax
import jax.numpy as jnp
from jax import lax
from jax.sharding import PartitionSpec as P


def in_one_piece(arrays, axis, split_dim, concat_dim, along):
    widths = [a.shape[along] for a in arrays]
    both = jnp.concatenate(arrays, axis=along)
    whole = lax.all_to_all(both, axis, split_axis=split_dim, concat_axis=concat_dim, tiled=True)
    return tuple(jnp.split(whole, [sum(widths[:k]) for k in range(1, len(widths))], axis=along))


def split_up(value, dim, devices):
    dims = value.shape
    tiles = value.reshape(*dims[:dim], devices, dims[dim] // devices, *dims[dim + 1 :])
    return jnp.moveaxis(tiles, dim, 0)


def sum_at_owner(value, axis, dim):
    devices = lax.axis_size(axis)
    tiles = lax.all_to_all(split_up(value, dim, devices), axis, 0, 0, tiled=True)
    return jnp.sum(tiles, axis=0)


def local(tokens, routing, gate_prob, up_weight, down_weight, out_grad):
    token_count = tokens.shape[0]
    local_experts = up_weight.shape[0]
    peer_count = lax.axis_size("ep")
    experts = local_experts * peer_count
    capacity = max(2, 2 * token_count // experts)
    slot_count = experts * capacity
    expert = routing[:, 0]
    onehot = (expert[:, None] == jnp.arange(experts, dtype=jnp.int32)[None, :]).astype(jnp.int32)
    ranking = jnp.sum((jnp.cumsum(onehot, axis=0) - onehot) * onehot, axis=1)
    target = expert * capacity + ranking
    placing = (jnp.arange(slot_count, dtype=jnp.int32)[:, None] == target[None, :]).astype(
        jnp.bfloat16
    )

    def dispatch(values):
        packed = jnp.dot(placing, values, preferred_element_type=jnp.float32).astype(jnp.bfloat16)
        return packed.reshape(experts, capacity, values.shape[1])

    def collect(returned):
        flat = returned.reshape(slot_count, returned.shape[2])
        return jnp.einsum("st,sd->td", placing, flat, preferred_element_type=jnp.float32)

    grad_wide = out_grad.astype(jnp.float32)
    scaled = (gate_prob[:, None] * grad_wide).astype(jnp.bfloat16)
    sent_rows, early_grads = in_one_piece((dispatch(tokens), dispatch(scaled)), "ep", 0, 1, 2)
    expert_rows = lax.all_gather(sent_rows, "dp", axis=1, tiled=True)
    up_full, down_full = (up_weight, down_weight)
    preact = jnp.einsum("erd,edf->erf", expert_rows, up_full, preferred_element_type=jnp.float32)
    activated, back_fn = jax.vjp(jax.nn.gelu, preact)
    hidden = activated.astype(jnp.bfloat16)
    partial_out = jnp.einsum("erf,efd->erd", hidden, down_full, preferred_element_type=jnp.float32)
    merged = sum_at_owner(partial_out, "dp", 1)
    expert_out = lax.all_to_all(
        merged.astype(jnp.bfloat16), "ep", split_axis=1, concat_axis=0, tiled=True
    )
    expert_tok = collect(expert_out)
    output = (gate_prob[:, None] * expert_tok).astype(jnp.bfloat16)
    prob_grad = jnp.sum(grad_wide * expert_tok, axis=1)
    grad_rows = lax.all_gather(early_grads, "dp", axis=1, tiled=True)
    hidden_grad = jnp.einsum(
        "erd,efd->erf", grad_rows, down_full, preferred_element_type=jnp.float32
    )
    preact_grad = back_fn(hidden_grad)[0].astype(jnp.bfloat16)
    partial_input = jnp.einsum(
        "erf,edf->erd", preact_grad, up_full, preferred_element_type=jnp.float32
    )
    up_sum = jnp.einsum(
        "erd,erf->edf", expert_rows, preact_grad, preferred_element_type=jnp.float32
    )
    down_sum = jnp.einsum("erf,erd->efd", hidden, grad_rows, preferred_element_type=jnp.float32)
    input_rows = sum_at_owner(partial_input, "dp", 1)
    up_grad = up_sum.astype(jnp.bfloat16)
    down_grad = down_sum.astype(jnp.bfloat16)
    returned = lax.all_to_all(
        input_rows.astype(jnp.bfloat16), "ep", split_axis=1, concat_axis=0, tiled=True
    )
    token_grad = collect(returned).astype(jnp.bfloat16)
    return (output, token_grad, prob_grad, up_grad, down_grad)


def solution(mesh):
    placed = (
        P(("ep", "dp"), None),
        P(("ep", "dp"), None),
        P(("ep", "dp")),
        P("ep", None, "dp"),
        P("ep", "dp", None),
        P(("ep", "dp"), None),
    )
    return jax.shard_map(
        local,
        mesh=mesh,
        in_specs=placed,
        out_specs=(
            P(("ep", "dp"), None),
            P(("ep", "dp"), None),
            P(("ep", "dp")),
            P("ep", None, "dp"),
            P("ep", "dp", None),
        ),
        check_vma=False,
    )
```

profile of v0, /device:TPU:32, one launch (start us, length us, event | category | flops | bytes accessed | tf_op | source)
XLA Modules:
  0.0 134.9 jit_solution(1658553204807080798)
XLA Ops:
  6.6 39.5 %all_to_all.40 = bf16[128,2,1536]{2,1,0:T(2,128)(2,1)} all-to-all(bf16[128,2,1536]{2,1,0:T(2,128)(2,1)S(1)} %pad_maximum_fusion), channel_id=1, replica_groups=mesh['ep'=128,'dp'=2] {'ep'}, dimensions={0} | all-to-all | bytes 1572864 | tf_op jit(solution)/shard_map/all_to_all | solution.py:10
  46.2 2.3 %all_to_all.13 = bf16[1,256,1536]{2,1,0:T(8,128)(2,1)S(1)} reshape(bf16[128,2,1536]{2,1,0:T(2,128)(2,1)} %all_to_all.40) | data formatting | bytes 1572864 | tf_op jit(solution)/shard_map/all_to_all | solution.py:10
  48.5 2.4 %all_gather.6 = bf16[1,512,768]{2,1,0:T(8,128)(2,1)S(1)} all-gather(bf16[1,256,768]{2,1,0:T(8,128)(2,1)S(1)} %get-tuple-element.6), channel_id=1, replica_groups=mesh['ep'=128,'dp'=2] {'dp'}, dimensions={1}, use_global_device_ids=true | all-gather | bytes 1179648 | tf_op jit(solution)/shard_map/all_gather | solution.py:52
  50.9 2.4 %all_gather.7 = bf16[1,512,768]{2,1,0:T(8,128)(2,1)S(1)} all-gather(bf16[1,256,768]{2,1,0:T(8,128)(2,1)S(1)} %get-tuple-element.5), channel_id=1, replica_groups=mesh['ep'=128,'dp'=2] {'dp'}, dimensions={1}, use_global_device_ids=true | all-gather | bytes 1179648 | tf_op jit(solution)/shard_map/all_gather | solution.py:65
  53.2 3.0 %multiply_convert_fusion = (bf16[512,1536]{1,0:T(8,128)(2,1)}, f32[512,1536]{1,0:T(8,128)S(1)}) fusion(bf16[1,768,1536]{2,1,0:T(8,128)(2,1)S(1)} %copy-done, bf16[1,512,768]{2,1,0:T(8,128)(2,1)S(1)} %all_gather.6), kind=kOutput, calls=%fused_computation.11 | convolution fusion | flops 1215037440 | bytes 7864320 | tf_op jit(solution)/shard_map/erd,edf->erf/dot_general | solution.py:54
  56.2 3.0 %fusion.6 = bf16[512,1536]{1,0:T(8,128)(2,1)S(1)} fusion(f32[512,1536]{1,0:T(8,128)S(1)} %get-tuple-element.10, bf16[1,1536,768]{2,1,0:T(8,128)(2,1)S(1)} %copy-done.5, bf16[1,512,768]{2,1,0:T(8,128)(2,1)S(1)} %all_gather.7), kind=kOutput, calls=%fused_computation.10 | convolution fusion | flops 1223688192 | bytes 7864320 | tf_op jit(solution)/shard_map/erd,efd->erf/dot_general | solution.py:66
  59.3 1.4 %fusion.22 = f32[2,1,256,768]{3,2,1,0:T(8,128)S(1)} fusion(bf16[2,256,1536]{2,1,0:T(8,128)(2,1)S(1)} %bitcast.84, bf16[1,768,1536]{2,1,0:T(8,128)(2,1)S(1)} %copy-done), kind=kOutput, calls=%fused_computation.23 | convolution fusion | flops 1207959552 | bytes 5505024 | tf_op jit(solution)/shard_map/erf,edf->erd/dot_general | solution.py:70
  60.7 5.8 %all_to_all.41 = f32[2,1,256,768]{3,2,1,0:T(8,128)} all-to-all(f32[2,1,256,768]{3,2,1,0:T(8,128)S(1)} %fusion.22), channel_id=1, replica_groups=mesh['ep'=128,'dp'=2] {'dp'}, dimensions={0} | all-to-all | bytes 3145728 | tf_op jit(solution)/shard_map/all_to_all | solution.py:22
  66.6 1.5 %reduce_sum.38 = bf16[256,768]{1,0:T(8,128)(2,1)S(1)} reduce(f32[2,1,256,768]{3,2,1,0:T(8,128)} %all_to_all.41, f32[]{:T(128)} %constant.19.clone.1), dimensions={0,1}, to_apply=%region_3.4 | reduce | flops 196608 | bytes 1966084 | tf_op jit(solution)/shard_map/reduce_sum | solution.py:23
  69.2 3.0 %reduce.3 = bf16[256,768]{1,0:T(8,128)(2,1)S(1)} reduce(bf16[256,1,768]{2,1,0:T(2,128)(2,1)S(1)} %bitcast.75, bf16[]{:T(256)} %broadcast.44), dimensions={1}, to_apply=%bitcast.73.reduce_sub_computation | reduce | bytes 786434
  73.1 3.5 %fusion.19 = f32[2,1,256,768]{3,2,1,0:T(8,128)S(1)} fusion(bf16[2,256,1536]{2,1,0:T(8,128)(2,1)} %bitcast.83, bf16[1,1536,768]{2,1,0:T(8,128)(2,1)} %param.10), kind=kOutput, calls=%fused_computation.22 | convolution fusion | flops 1207959552 | bytes 5505024 | tf_op jit(solution)/shard_map/erf,efd->erd/dot_general | solution.py:57
  76.7 5.8 %all_to_all.42 = f32[2,1,256,768]{3,2,1,0:T(8,128)} all-to-all(f32[2,1,256,768]{3,2,1,0:T(8,128)S(1)} %fusion.19), channel_id=1, replica_groups=mesh['ep'=128,'dp'=2] {'dp'}, dimensions={0} | all-to-all | bytes 3145728 | tf_op jit(solution)/shard_map/all_to_all | solution.py:22
  82.5 7.2 %all-to-all-start.4 = ((bf16[128,2,768]{2,1,0:T(2,128)(2,1)}), bf16[128,2,768]{2,1,0:T(2,128)(2,1)S(1)}, u32[]{:S(2)}, u32[]{:S(2)}) async-start(bf16[128,2,768]{2,1,0:T(2,128)(2,1)} %reshape.147), calls=%async_computation.4 | async-start | bytes 786432 | tf_op jit(solution)/shard_map/all_to_all | solution.py:80
  89.7 2.4 %reduce_sum.37 = bf16[256,768]{1,0:T(8,128)(2,1)} reduce(f32[2,1,256,768]{3,2,1,0:T(8,128)} %all_to_all.42, f32[]{:T(128)} %constant.19.clone.1), dimensions={0,1}, to_apply=%region_2.3 | reduce | flops 196608 | bytes 1966084 | tf_op jit(solution)/shard_map/reduce_sum | solution.py:23
  92.1 1.6 %copy.32 = bf16[1,256,768]{2,0,1:T(2,128)(2,1)S(1)} copy(bf16[1,256,768]{2,1,0:T(8,128)(2,1)} %bitcast.78) | data formatting | bytes 786432 | tf_op jit(solution)/shard_map/convert_element_type | solution.py:60
  93.7 3.8 %reduce.2 = bf16[256,768]{1,0:T(8,128)(2,1)} reduce(bf16[256,1,768]{2,1,0:T(2,128)(2,1)S(1)} %bitcast.76, bf16[]{:T(256)} %broadcast.44), dimensions={1}, to_apply=%bitcast.74.reduce_sub_computation | reduce | bytes 786434
  97.4 1.9 %reshape.145 = bf16[128,2,768]{2,1,0:T(2,128)(2,1)} reshape(bf16[256,768]{1,0:T(8,128)(2,1)} %reduce.2) | data formatting | bytes 786432
  99.3 7.3 %all-to-all-done.4 = bf16[128,2,768]{2,1,0:T(2,128)(2,1)S(1)} async-done(((bf16[128,2,768]{2,1,0:T(2,128)(2,1)}), bf16[128,2,768]{2,1,0:T(2,128)(2,1)S(1)}, u32[]{:S(2)}, u32[]{:S(2)}) %all-to-all-start.4) | async-done | bytes 393248 | tf_op jit(solution)/shard_map/all_to_all | solution.py:80
  106.6 7.5 %all-to-all-start.2 = ((bf16[128,2,768]{2,1,0:T(2,128)(2,1)}), bf16[128,2,768]{2,1,0:T(2,128)(2,1)}, u32[]{:S(2)}, u32[]{:S(2)}) async-start(bf16[128,2,768]{2,1,0:T(2,128)(2,1)} %reshape.145), calls=%async_computation.2 | async-start | bytes 786432 | tf_op jit(solution)/shard_map/all_to_all | solution.py:59
  114.2 4.6 %fusion.7 = bf16[1,768,1536]{2,1,0:T(8,128)(2,1)} fusion(bf16[512,1536]{1,0:T(8,128)(2,1)} %copy-done.7, bf16[1,512,768]{2,1,0:T(8,128)(2,1)} %copy-done.1), kind=kOutput, calls=%fused_computation.12 | convolution fusion | flops 1209139200 | bytes 4718592 | tf_op jit(solution)/shard_map/erd,erf->edf/dot_general | solution.py:73
  118.8 2.8 %fusion.8 = bf16[1,1536,768]{2,1,0:T(8,128)(2,1)} fusion(bf16[512,1536]{1,0:T(8,128)(2,1)S(1)} %copy-done.6, bf16[1,512,768]{2,1,0:T(8,128)(2,1)S(1)} %copy-done.3), kind=kOutput, calls=%fused_computation.13 | convolution fusion | flops 1209139200 | bytes 4718592 | tf_op jit(solution)/shard_map/erf,erd->efd/dot_general | solution.py:76
  122.9 6.8 %all-to-all-done.2 = bf16[128,2,768]{2,1,0:T(2,128)(2,1)} async-done(((bf16[128,2,768]{2,1,0:T(2,128)(2,1)}), bf16[128,2,768]{2,1,0:T(2,128)(2,1)}, u32[]{:S(2)}, u32[]{:S(2)}) %all-to-all-start.2) | async-done | bytes 393248 | tf_op jit(solution)/shard_map/all_to_all | solution.py:59
  129.7 2.7 %reshape.146 = bf16[256,1,768]{2,1,0:T(2,128)(2,1)S(1)} reshape(bf16[128,2,768]{2,1,0:T(2,128)(2,1)} %all-to-all-done.2) | data formatting | bytes 786432
  132.4 2.5 %fusion.30 = (f32[128]{0:T(128)}, bf16[128,768]{1,0:T(8,128)(2,1)}) fusion(bf16[128,768]{1,0:T(8,128)(2,1)} %param.11, f32[128]{0:T(128)S(1)} %copy-done.4, bf16[1,256,768]{2,0,1:T(2,128)(2,1)S(1)} %bitcast.80, s32[128]{0:T(128)S(1)} %multiply_add_fusion), kind=kOutput, calls=%fused_computation.35 | convolution fusion | flops 50855808 | bytes 787968 | tf_op jit(solution)/shard_map/st,sd->td/dot_general | solution.py:47
  (31 shorter events, 9.3 us)
Async XLA Ops:
  0.6 52.6 %copy-start = (bf16[1,768,1536]{2,1,0:T(8,128)(2,1)S(1)}, bf16[1,768,1536]{2,1,0:T(8,128)(2,1)}, u32[]{:S(2)}) copy-start(bf16[1,768,1536]{2,1,0:T(8,128)(2,1)} %param.9) | copy-start | bytes 7077892
  50.9 5.4 %copy-start.1 = (bf16[1,512,768]{2,1,0:T(8,128)(2,1)}, bf16[1,512,768]{2,1,0:T(8,128)(2,1)S(1)}, u32[]{:S(2)}) copy-start(bf16[1,512,768]{2,1,0:T(8,128)(2,1)S(1)} %all_gather.6) | copy-start | bytes 2359300
  53.2 3.0 %copy-start.2 = (bf16[1,512,768]{2,1,0:T(8,128)(2,1)}, bf16[1,512,768]{2,1,0:T(8,128)(2,1)S(1)}, u32[]{:S(2)}) copy-start(bf16[1,512,768]{2,1,0:T(8,128)(2,1)S(1)} %all_gather.7) | copy-start | bytes 2359300
  53.2 3.0 %copy-start.5 = (bf16[1,1536,768]{2,1,0:T(8,128)(2,1)S(1)}, bf16[1,1536,768]{2,1,0:T(8,128)(2,1)}, u32[]{:S(2)}) copy-start(bf16[1,1536,768]{2,1,0:T(8,128)(2,1)} %param.10) | copy-start | bytes 7077892
  59.3 1.4 %copy-start.7 = (bf16[512,1536]{1,0:T(8,128)(2,1)}, bf16[512,1536]{1,0:T(8,128)(2,1)S(1)}, u32[]{:S(2)}) copy-start(bf16[512,1536]{1,0:T(8,128)(2,1)S(1)} %fusion.6) | copy-start | bytes 4718596
  82.5 24.1 %all-to-all-start.4 = ((bf16[128,2,768]{2,1,0:T(2,128)(2,1)}), bf16[128,2,768]{2,1,0:T(2,128)(2,1)S(1)}, u32[]{:S(2)}, u32[]{:S(2)}) async-start(bf16[128,2,768]{2,1,0:T(2,128)(2,1)} %reshape.147), calls=%async_computation.4 | async-start | bytes 786432 | tf_op jit(solution)/shard_map/all_to_all | solution.py:80
  106.6 23.1 %all-to-all-start.2 = ((bf16[128,2,768]{2,1,0:T(2,128)(2,1)}), bf16[128,2,768]{2,1,0:T(2,128)(2,1)}, u32[]{:S(2)}, u32[]{:S(2)}) async-start(bf16[128,2,768]{2,1,0:T(2,128)(2,1)} %reshape.145), calls=%async_computation.2 | async-start | bytes 786432 | tf_op jit(solution)/shard_map/all_to_all | solution.py:59
  114.1 4.6 %copy-start.3 = (bf16[1,512,768]{2,1,0:T(8,128)(2,1)S(1)}, bf16[1,512,768]{2,1,0:T(8,128)(2,1)}, u32[]{:S(2)}) copy-start(bf16[1,512,768]{2,1,0:T(8,128)(2,1)} %copy-done.2) | copy-start | bytes 2359300
  114.1 4.6 %copy-start.6 = (bf16[512,1536]{1,0:T(8,128)(2,1)S(1)}, bf16[512,1536]{1,0:T(8,128)(2,1)}, u32[]{:S(2)}) copy-start(bf16[512,1536]{1,0:T(8,128)(2,1)} %get-tuple-element.9) | copy-start | bytes 4718596
  118.8 13.6 %copy-start.4 = (f32[128]{0:T(128)S(1)}, f32[128]{0:T(128)}, u32[]{:S(2)}) copy-start(f32[128]{0:T(128)} %param.8) | copy-start | bytes 1540
where the time goes:
time: 136 us; the launch traced here: 135 us
  blocking collectives  55.9 us (41%)
  matrix products  24.2 us (18%)
  starting transfers between devices  14.7 us (11%)
  waiting for transfers between devices  14.1 us (10%)
  other arithmetic  13.9 us (10%)
  local copies, waits for them, and re-layouts  11.2 us (8%)
    all_to_all x1, blocking collectives, in_one_piece(): lax.all_to_all(both, axis, split_axis=split_dim, concat_axis=concat_dim,...  39.5 us
    all_to_all x2, blocking collectives, sum_at_owner(): lax.all_to_all(split_up(value, dim, devices), axis, 0, 0, tiled=True)  11.7 us
    all_to_all x1, starting transfers between devices, local(): lax.all_to_all(merged.astype(jnp.bfloat16), 'ep', split_axis=1, concat_ax...  7.52 us
    all_to_all x1, waiting for transfers between devices, local(): lax.all_to_all(input_rows.astype(jnp.bfloat16), 'ep', split_axis=1, conca...  7.29 us
    all_to_all x1, starting transfers between devices, local(): lax.all_to_all(input_rows.astype(jnp.bfloat16), 'ep', split_axis=1, conca...  7.18 us
    all_to_all x1, waiting for transfers between devices, local(): lax.all_to_all(merged.astype(jnp.bfloat16), 'ep', split_axis=1, concat_ax...  6.8 us
    unnamed x2, other arithmetic  6.76 us
    unnamed x21, local copies, waits for them, and re-layouts  6.36 us
  transfers between devices with their start and end apart: 2, of which 2 were waited for; matrix products, arithmetic and copies ran while one was open for 14% of the time, Pallas kernels for 0%

commit v1 on v0

v1 whole, which is shorter than its diff:
```python
import jax
import jax.numpy as jnp
from jax import lax
from jax.sharding import PartitionSpec as P


def local(tokens, routing, gate_prob, up_weight, down_weight, out_grad):
    token_count, width = tokens.shape
    experts = up_weight.shape[0] * lax.axis_size("ep")
    capacity = max(2, 2 * token_count // experts)
    slots = experts * capacity

    def swap(value):
        return lax.ppermute(value, "dp", [(0, 1), (1, 0)])

    up_own, down_own = up_weight[0], down_weight[0]
    up_far, down_far = swap(up_own), swap(down_own)

    expert = routing[:, 0]
    earlier = jnp.arange(token_count)[:, None] > jnp.arange(token_count)[None, :]
    same = (expert[:, None] == expert[None, :]) & earlier
    target = expert * capacity + jnp.sum(same.astype(jnp.int32), axis=1)
    placing = (jnp.arange(slots, dtype=jnp.int32)[:, None] == target[None, :]).astype(jnp.bfloat16)
    grad_wide = out_grad.astype(jnp.float32)
    scaled = (gate_prob[:, None] * grad_wide).astype(jnp.bfloat16)
    both = jnp.concatenate([tokens, scaled], axis=1)
    packed = jnp.dot(placing, both, preferred_element_type=jnp.float32).astype(jnp.bfloat16)

    def exchange(value):
        value = value.reshape(experts, capacity, 2 * width)
        return lax.all_to_all(value, "ep", 0, 0, tiled=True).reshape(slots, 2 * width)

    received = exchange(packed)
    rows, grads = received[:, :width], received[:, width:]
    dot = lambda a, b, dims: lax.dot_general(
        a, b, ((dims[:1], dims[1:]), ((), ())), preferred_element_type=jnp.float32
    )

    def half(up, down):
        preact = dot(rows, up, (1, 0))
        activated, back_fn = jax.vjp(jax.nn.gelu, preact)
        hidden = activated.astype(jnp.bfloat16)
        hidden_grad = dot(grads, down, (1, 1))
        preact_grad = back_fn(hidden_grad)[0].astype(jnp.bfloat16)
        return hidden, preact_grad

    hidden_own, preact_grad_own = half(up_own, down_own)
    hidden_far, preact_grad_far = half(up_far, down_far)
    result = dot(hidden_own, down_own, (1, 0)) + dot(hidden_far, down_far, (1, 0))
    token_side = dot(preact_grad_own, up_own, (1, 1)) + dot(preact_grad_far, up_far, (1, 1))
    sent_back = jnp.concatenate([result, token_side], axis=1).astype(jnp.bfloat16)
    returned = exchange(sent_back)

    received_far = swap(received)
    hidden_near, preact_grad_near = swap(hidden_far), swap(preact_grad_far)
    rows_all = jnp.concatenate([rows, received_far[:, :width]], axis=0)
    grads_all = jnp.concatenate([grads, received_far[:, width:]], axis=0)
    hidden_all = jnp.concatenate([hidden_own, hidden_near], axis=0)
    preact_grad_all = jnp.concatenate([preact_grad_own, preact_grad_near], axis=0)
    up_grad = dot(rows_all, preact_grad_all, (0, 0)).astype(jnp.bfloat16)[None]
    down_grad = dot(hidden_all, grads_all, (0, 0)).astype(jnp.bfloat16)[None]

    collected = dot(placing, returned, (0, 0))
    expert_tok = collected[:, :width]
    output = (gate_prob[:, None] * expert_tok).astype(jnp.bfloat16)
    prob_grad = jnp.sum(grad_wide * expert_tok, axis=1)
    token_grad = collected[:, width:].astype(jnp.bfloat16)
    return (output, token_grad, prob_grad, up_grad, down_grad)


def solution(mesh):
    rows = P(("ep", "dp"), None)
    flat = P(("ep", "dp"))
    up, down = P("ep", None, "dp"), P("ep", "dp", None)
    return jax.shard_map(
        local,
        mesh=mesh,
        in_specs=(rows, rows, flat, up, down, rows),
        out_specs=(rows, rows, flat, up, down),
        check_vma=False,
    )
```

time: 136 us -> 100 us (0.74)
  blocking collectives: 55.9 us -> 0 us
  waiting for transfers between devices: 14.1 us -> 41.3 us
  starting transfers between devices: 14.7 us -> 23.6 us
  other arithmetic: 13.9 us -> 5.51 us
  local copies, waits for them, and re-layouts: 11.2 us -> 3.45 us
    all_to_all x3 -> x0, blocking collectives: 51.2 us -> none  [the longest x1 39.5 us: in_one_piece(): lax.all_to_all(both, axis, split_axis=split_dim, concat_axis=concat_dim,...]
    all_to_all x2, waiting for transfers between devices: 14.1 us -> 38.6 us  [exchange(): lax.all_to_all(value, 'ep', 0, 0, tiled=True).reshape(slots, 2 * width)]
    all_to_all x2, starting transfers between devices: 14.7 us -> 22.4 us  [exchange(): lax.all_to_all(value, 'ep', 0, 0, tiled=True).reshape(slots, 2 * width)]
    unnamed x2 -> x0, other arithmetic: 6.76 us -> none
    unnamed x21 -> x16, local copies, waits for them, and re-layouts: 6.36 us -> 0.58 us
    all_gather x2 -> x0, blocking collectives: 4.73 us -> none  [the longest x1 2.37 us: local(): expert_rows = lax.all_gather(sent_rows, 'dp', axis=1, tiled=True)]
    ppermute x0 -> x5, waiting for transfers between devices: none -> 2.7 us  [swap(): return lax.ppermute(value, 'dp', [(0, 1), (1, 0)])]
    reduce_sum x3 -> x2, other arithmetic: 4.73 us -> 2.2 us  [the longest x1 1.3 us: local(): prob_grad = jnp.sum(grad_wide * expert_tok, axis=1)]
  transfers between devices with their start and end apart: 2 -> 7, of which waited for: 2 -> 4; matrix products, arithmetic and copies ran while one was open for 14% -> 15% of each run, Pallas kernels for 0% -> 0%
where the time goes in v1:
time: 100 us; the launch traced here: 99.5 us
  waiting for transfers between devices  41.3 us (41%)
  matrix products  24.8 us (25%)
  starting transfers between devices  23.6 us (24%)
  other arithmetic  5.51 us (6%)
  local copies, waits for them, and re-layouts  3.45 us (3%)
    all_to_all x2, waiting for transfers between devices, exchange(): lax.all_to_all(value, 'ep', 0, 0, tiled=True).reshape(slots, 2 * width)  38.6 us
    dot_general x11, matrix products, local(): lax.dot_general(a, b, ((dims[:1], dims[1:]), ((), ())), preferred_element...  23.5 us
    all_to_all x2, starting transfers between devices, exchange(): lax.all_to_all(value, 'ep', 0, 0, tiled=True).reshape(slots, 2 * width)  22.4 us
    ppermute x5, waiting for transfers between devices, swap(): return lax.ppermute(value, 'dp', [(0, 1), (1, 0)])  2.7 us
  transfers between devices with their start and end apart: 7, of which 4 were waited for; matrix products, arithmetic and copies ran while one was open for 15% of the time, Pallas kernels for 0%

profile of v1, /device:TPU:32, one launch (start us, length us, event | category | flops | bytes accessed | tf_op | source)
XLA Modules:
  0.0 99.5 jit_solution(10826453096154537378)
XLA Ops:
  0.6 0.9 convert_reduce_fusion
  1.5 0.7 multiply_add_fusion
  2.2 1.0 %fusion.30 = bf16[128,768]{1,0:T(8,128)(2,1)S(1)} fusion(bf16[128,768]{1,0:T(8,128)(2,1)} %param.11, f32[128]{0:T(128)} %param.8), kind=kLoop, calls=%fused_computation.44 | loop fusion | flops 294912 | bytes 393728 | tf_op jit(solution)/shard_map/convert_element_type | solution.py:25
  3.2 1.3 %convolution_convert_fusion.2 = bf16[256,1536]{1,0:T(8,128)(2,1)S(1)} fusion(bf16[128,768]{1,0:T(8,128)(2,1)S(1)} %fusion.30, bf16[128,768]{1,0:T(8,128)(2,1)} %param.6, s32[128]{0:T(128)S(1)} %multiply_add_fusion), kind=kOutput, calls=%fused_computation.4 | convolution fusion | flops 101875712 | bytes 1180160 | tf_op jit(solution)/shard_map/dot_general | solution.py:27
  4.5 1.2 %reshape.34 = bf16[128,2,1536]{2,1,0:T(2,128)(2,1)} reshape(bf16[256,1536]{1,0:T(8,128)(2,1)S(1)} %convolution_convert_fusion.2) | data formatting | bytes 1572864 | tf_op jit(solution)/shard_map/reshape | solution.py:30
  5.7 15.0 %all-to-all-start = ((bf16[128,2,1536]{2,1,0:T(2,128)(2,1)}), bf16[128,2,1536]{2,1,0:T(2,128)(2,1)S(1)}, u32[]{:S(2)}, u32[]{:S(2)}) async-start(bf16[128,2,1536]{2,1,0:T(2,128)(2,1)} %reshape.34), calls=%async_computation | async-start | bytes 1572864 | tf_op jit(solution)/shard_map/all_to_all | solution.py:31
  21.3 24.0 %all-to-all-done = bf16[128,2,1536]{2,1,0:T(2,128)(2,1)S(1)} async-done(((bf16[128,2,1536]{2,1,0:T(2,128)(2,1)}), bf16[128,2,1536]{2,1,0:T(2,128)(2,1)S(1)}, u32[]{:S(2)}, u32[]{:S(2)}) %all-to-all-start) | async-done | bytes 786464 | tf_op jit(solution)/shard_map/all_to_all | solution.py:31
  45.6 2.8 %multiply_convert_fusion.1 = (bf16[256,1536]{1,0:T(8,128)(2,1)S(1)}, f32[256,1536]{1,0:T(8,128)S(1)}) fusion(bf16[1,768,1536]{2,1,0:T(8,128)(2,1)} %param.9, bf16[256,1536]{1,0:T(8,128)(2,1)S(1)} %reshape.35), kind=kOutput, calls=%fused_computation.30 | convolution fusion | flops 607518720 | bytes 5111808 | tf_op jit(solution)/shard_map/dot_general | solution.py:35
  48.5 1.5 %fusion.8 = bf16[256,1536]{1,0:T(8,128)(2,1)S(1)} fusion(f32[256,1536]{1,0:T(8,128)S(1)} %get-tuple-element.12, bf16[1,1536,768]{2,1,0:T(8,128)(2,1)S(1)} %copy-done.3, bf16[256,1536]{1,0:T(8,128)(2,1)S(1)} %reshape.35), kind=kOutput, calls=%fused_computation.15 | convolution fusion | flops 611844096 | bytes 5111808 | tf_op jit(solution)/shard_map/dot_general | solution.py:35
  50.4 0.8 fusion.48
  51.3 1.7 %fusion.44 = f32[256,768]{1,0:T(8,128)} fusion(bf16[256,1536]{1,0:T(8,128)(2,1)S(1)} %get-tuple-element.11, bf16[1,1536,768]{2,1,0:T(8,128)(2,1)S(1)} %copy-done.3), kind=kOutput, calls=%fused_computation.64 | convolution fusion | flops 603979776 | bytes 3932160 | tf_op jit(solution)/shard_map/dot_general | solution.py:35
  52.9 2.6 %multiply_convert_fusion = (bf16[256,1536]{1,0:T(8,128)(2,1)S(1)}, f32[256,1536]{1,0:T(8,128)S(1)}) fusion(bf16[768,1536]{1,0:T(8,128)(2,1)} %collective-permute-done, bf16[256,1536]{1,0:T(8,128)(2,1)S(1)} %reshape.35), kind=kOutput, calls=%fused_computation.29 | convolution fusion | flops 607518720 | bytes 5111808 | tf_op jit(solution)/shard_map/dot_general | solution.py:35
  55.6 3.1 %fusion.15 = bf16[256,1536]{1,0:T(8,128)(2,1)S(1)} fusion(f32[256,1536]{1,0:T(8,128)S(1)} %get-tuple-element.14, bf16[1536,768]{1,0:T(8,128)(2,1)} %collective-permute-done.1, bf16[256,1536]{1,0:T(8,128)(2,1)S(1)} %reshape.35), kind=kOutput, calls=%fused_computation.22 | convolution fusion | flops 611844096 | bytes 5111808 | tf_op jit(solution)/shard_map/dot_general | solution.py:35
  58.7 2.5 %fusion.23 = bf16[256,768]{1,0:T(8,128)(2,1)S(1)} fusion(f32[256,768]{1,0:T(8,128)S(1)} %fusion.48, bf16[256,1536]{1,0:T(8,128)(2,1)S(1)} %fusion.15, bf16[768,1536]{1,0:T(8,128)(2,1)} %collective-permute-done), kind=kOutput, calls=%fused_computation.34 | convolution fusion | flops 604372992 | bytes 4325376 | tf_op jit(solution)/shard_map/dot_general | solution.py:35
  61.4 2.6 %fusion.22 = bf16[256,768]{1,0:T(8,128)(2,1)S(1)} fusion(f32[256,768]{1,0:T(8,128)} %fusion.44, bf16[256,1536]{1,0:T(8,128)(2,1)S(1)} %get-tuple-element.13, bf16[1536,768]{1,0:T(8,128)(2,1)} %collective-permute-done.1), kind=kOutput, calls=%fused_computation.33 | convolution fusion | flops 604372992 | bytes 4325376 | tf_op jit(solution)/shard_map/dot_general | solution.py:35
  64.2 1.6 %pad_maximum_fusion = bf16[128,2,1536]{2,1,0:T(2,128)(2,1)} fusion(bf16[128,2,768]{2,1,0:T(2,128)(2,1)S(1)} %concatenate.26, bf16[128,2,768]{2,1,0:T(2,128)(2,1)S(1)} %concatenate.25), kind=kLoop, calls=%fused_computation.35 | loop fusion | flops 1572864 | bytes 1572864 | tf_op jit(solution)/shard_map/concatenate | solution.py:51
  65.8 7.4 %all-to-all-start.1 = ((bf16[128,2,1536]{2,1,0:T(2,128)(2,1)}), bf16[128,2,1536]{2,1,0:T(2,128)(2,1)S(1)}, u32[]{:S(2)}, u32[]{:S(2)}) async-start(bf16[128,2,1536]{2,1,0:T(2,128)(2,1)} %pad_maximum_fusion), calls=%async_computation.1 | async-start | bytes 1572864 | tf_op jit(solution)/shard_map/all_to_all | solution.py:31
  73.9 1.6 %collective-permute-done.2 = bf16[256,1536]{1,0:T(8,128)(2,1)S(1)} collective-permute-done((bf16[256,1536]{1,0:T(8,128)(2,1)S(1)}, bf16[256,1536]{1,0:T(8,128)(2,1)S(1)}, u32[]{:S(2)}, u32[]{:S(2)}) %collective-permute-start.2) | collective-permute-done | bytes 786464 | tf_op jit(solution)/shard_map/ppermute | solution.py:14
  75.6 1.1 %collective-permute-done.3 = bf16[256,1536]{1,0:T(8,128)(2,1)S(1)} collective-permute-done((bf16[256,1536]{1,0:T(8,128)(2,1)S(1)}, bf16[256,1536]{1,0:T(8,128)(2,1)S(1)}, u32[]{:S(2)}, u32[]{:S(2)}) %collective-permute-start.3) | collective-permute-done | bytes 786464 | tf_op jit(solution)/shard_map/ppermute | solution.py:14
  76.6 2.8 %fusion = bf16[1,768,1536]{2,1,0:T(8,128)(2,1)} fusion(bf16[256,1536]{1,0:T(8,128)(2,1)S(1)} %collective-permute-done.3, bf16[256,1536]{1,0:T(8,128)(2,1)S(1)} %copy-done.7, bf16[256,768]{1,0:T(8,128)(2,1)S(1)} %get-tuple-element.8, bf16[256,768]{1,0:T(8,128)(2,1)S(1)} %get-tuple-element.6), kind=kOutput, calls=%fused_computation.2 | convolution fusion | flops 1213857792 | bytes 4718592 | tf_op jit(solution)/shard_map/dot_general | solution.py:35
  79.5 2.8 %fusion.1 = bf16[1,1536,768]{2,1,0:T(8,128)(2,1)} fusion(bf16[256,1536]{1,0:T(8,128)(2,1)S(1)} %collective-permute-done.4, bf16[256,1536]{1,0:T(8,128)(2,1)S(1)} %copy-done.5, bf16[256,768]{1,0:T(8,128)(2,1)S(1)} %get-tuple-element.7, bf16[256,768]{1,0:T(8,128)(2,1)S(1)} %get-tuple-element.5), kind=kOutput, calls=%fused_computation.3 | convolution fusion | flops 1213857792 | bytes 4718592 | tf_op jit(solution)/shard_map/dot_general | solution.py:35
  82.3 14.6 %all-to-all-done.1 = bf16[128,2,1536]{2,1,0:T(2,128)(2,1)S(1)} async-done(((bf16[128,2,1536]{2,1,0:T(2,128)(2,1)}), bf16[128,2,1536]{2,1,0:T(2,128)(2,1)S(1)}, u32[]{:S(2)}, u32[]{:S(2)}) %all-to-all-start.1) | async-done | bytes 786464 | tf_op jit(solution)/shard_map/all_to_all | solution.py:31
  97.5 1.3 %fusion.31 = (f32[128]{0:T(128)}, bf16[128,768]{1,0:T(8,128)(2,1)}) fusion(bf16[128,768]{1,0:T(8,128)(2,1)S(1)} %copy-done, f32[128,1536]{1,0:T(8,128)S(1)} %fusion.35, f32[128]{0:T(128)S(1)} %copy-done.1), kind=kLoop, calls=%fused_computation.45 | loop fusion | flops 491392 | bytes 787456 | tf_op jit(solution)/shard_map/reduce_sum | solution.py:66
  98.8 0.7 slice.44
  (31 shorter events, 3.2 us)
Async XLA Ops:
  5.7 39.6 %all-to-all-start = ((bf16[128,2,1536]{2,1,0:T(2,128)(2,1)}), bf16[128,2,1536]{2,1,0:T(2,128)(2,1)S(1)}, u32[]{:S(2)}, u32[]{:S(2)}) async-start(bf16[128,2,1536]{2,1,0:T(2,128)(2,1)} %reshape.34), calls=%async_computation | async-start | bytes 1572864 | tf_op jit(solution)/shard_map/all_to_all | solution.py:31
  20.7 32.2 %collective-permute-start = (bf16[768,1536]{1,0:T(8,128)(2,1)}, bf16[768,1536]{1,0:T(8,128)(2,1)}, u32[]{:S(2)}, u32[]{:S(2)}) collective-permute-start(bf16[768,1536]{1,0:T(8,128)(2,1)} %bitcast.29), channel_id=1, source_target_pairs={{0,1},{1,0},{2,3},{3,2},{4,5},{5,4},{6,7},{7,6},{8,9},{9,8},{10,11... | collective-permute-start | bytes 7077896 | tf_op jit(solution)/shard_map/ppermute | solution.py:14
  20.8 34.8 %collective-permute-start.1 = (bf16[1536,768]{1,0:T(8,128)(2,1)}, bf16[1536,768]{1,0:T(8,128)(2,1)}, u32[]{:S(2)}, u32[]{:S(2)}) collective-permute-start(bf16[1536,768]{1,0:T(8,128)(2,1)} %bitcast.30), channel_id=1, source_target_pairs={{0,1},{1,0},{2,3},{3,2},{4,5},{5,4},{6,7},{7,6},{8,9},{9,8},{10,11... | collective-permute-start | bytes 7077896 | tf_op jit(solution)/shard_map/ppermute | solution.py:14
  45.6 2.8 %copy-start.3 = (bf16[1,1536,768]{2,1,0:T(8,128)(2,1)S(1)}, bf16[1,1536,768]{2,1,0:T(8,128)(2,1)}, u32[]{:S(2)}) copy-start(bf16[1,1536,768]{2,1,0:T(8,128)(2,1)} %param.10) | copy-start | bytes 7077892
  48.4 2.9 %copy-start.4 = (bf16[256,1536]{1,0:T(8,128)(2,1)}, bf16[256,1536]{1,0:T(8,128)(2,1)S(1)}, u32[]{:S(2)}) copy-start(bf16[256,1536]{1,0:T(8,128)(2,1)S(1)} %get-tuple-element.11) | copy-start | bytes 2359300
  48.5 2.0 %copy-start.2 = (bf16[1,768,1536]{2,1,0:T(8,128)(2,1)S(1)}, bf16[1,768,1536]{2,1,0:T(8,128)(2,1)}, u32[]{:S(2)}) copy-start(bf16[1,768,1536]{2,1,0:T(8,128)(2,1)} %param.9) | copy-start | bytes 7077892
  50.4 0.9 copy-start.6
  65.8 31.1 %all-to-all-start.1 = ((bf16[128,2,1536]{2,1,0:T(2,128)(2,1)}), bf16[128,2,1536]{2,1,0:T(2,128)(2,1)S(1)}, u32[]{:S(2)}, u32[]{:S(2)}) async-start(bf16[128,2,1536]{2,1,0:T(2,128)(2,1)} %pad_maximum_fusion), calls=%async_computation.1 | async-start | bytes 1572864 | tf_op jit(solution)/shard_map/all_to_all | solution.py:31
  73.1 3.5 %copy-start.7 = (bf16[256,1536]{1,0:T(8,128)(2,1)S(1)}, bf16[256,1536]{1,0:T(8,128)(2,1)}, u32[]{:S(2)}) copy-start(bf16[256,1536]{1,0:T(8,128)(2,1)} %copy-done.6) | copy-start | bytes 2359300
  73.1 2.4 %collective-permute-start.2 = (bf16[256,1536]{1,0:T(8,128)(2,1)S(1)}, bf16[256,1536]{1,0:T(8,128)(2,1)S(1)}, u32[]{:S(2)}, u32[]{:S(2)}) collective-permute-start(bf16[256,1536]{1,0:T(8,128)(2,1)S(1)} %reshape.35), channel_id=1, source_target_pairs={{0,1},{1,0},{2,3},{3,2},{4,5},{5,4},{6,7},{7,6},{8,9},{9,8},{10,11... | collective-permute-start | bytes 2359304 | tf_op jit(solution)/shard_map/ppermute | solution.py:14
  73.2 3.4 %collective-permute-start.3 = (bf16[256,1536]{1,0:T(8,128)(2,1)S(1)}, bf16[256,1536]{1,0:T(8,128)(2,1)S(1)}, u32[]{:S(2)}, u32[]{:S(2)}) collective-permute-start(bf16[256,1536]{1,0:T(8,128)(2,1)S(1)} %fusion.15), channel_id=1, source_target_pairs={{0,1},{1,0},{2,3},{3,2},{4,5},{5,4},{6,7},{7,6},{8,9},{9,8},{10,11... | collective-permute-start | bytes 2359304 | tf_op jit(solution)/shard_map/ppermute | solution.py:14
  73.7 5.7 %collective-permute-start.4 = (bf16[256,1536]{1,0:T(8,128)(2,1)S(1)}, bf16[256,1536]{1,0:T(8,128)(2,1)S(1)}, u32[]{:S(2)}, u32[]{:S(2)}) collective-permute-start(bf16[256,1536]{1,0:T(8,128)(2,1)S(1)} %get-tuple-element.13), channel_id=1, source_target_pairs={{0,1},{1,0},{2,3},{3,2},{4,5},{5,4},{6,7},{7,6},{8,9},{9,8},{10,11... | collective-permute-start | bytes 2359304 | tf_op jit(solution)/shard_map/ppermute | solution.py:14
  76.6 2.8 %copy-start.5 = (bf16[256,1536]{1,0:T(8,128)(2,1)S(1)}, bf16[256,1536]{1,0:T(8,128)(2,1)}, u32[]{:S(2)}) copy-start(bf16[256,1536]{1,0:T(8,128)(2,1)} %copy-done.4) | copy-start | bytes 2359300
  82.3 15.2 %copy-start = (bf16[128,768]{1,0:T(8,128)(2,1)S(1)}, bf16[128,768]{1,0:T(8,128)(2,1)}, u32[]{:S(2)}) copy-start(bf16[128,768]{1,0:T(8,128)(2,1)} %param.11) | copy-start | bytes 589828
  82.3 15.2 %copy-start.1 = (f32[128]{0:T(128)S(1)}, f32[128]{0:T(128)}, u32[]{:S(2)}) copy-start(f32[128]{0:T(128)} %param.8) | copy-start | bytes 1540

commit v2 on v1

v2 whole, which is shorter than its diff:
```python
import functools
import math

import jax
import jax.numpy as jnp
from jax import lax
from jax.experimental import pallas as pl
from jax.experimental.pallas import tpu as pltpu
from jax.sharding import PartitionSpec as P

F32 = jnp.float32
BF16 = jnp.bfloat16
GELU_SLOPE = math.sqrt(2.0 / math.pi)
GELU_CUBIC = 0.044715
PIECES = 4
BLOCK = 256


def dot(a, b, dims):
    return lax.dot_general(a, b, ((dims[:1], dims[1:]), ((), ())), preferred_element_type=F32)


def iota(shape, dim):
    return lax.broadcasted_iota(jnp.int32, shape, dim)


def columns(row, n):
    return jnp.transpose(jnp.broadcast_to(row, (n, n)))


def near(value):
    return pltpu.with_memory_space_constraint(value, pltpu.VMEM)


def far(value):
    return pltpu.with_memory_space_constraint(value, pltpu.HBM)


def prep_body(tokens_ref, routing_ref, gate_ref, grad_ref, packed_ref, target_ref):
    n, width = tokens_ref.shape
    piece = width // 2
    expert_row = routing_ref[...]
    same = (columns(expert_row, n) == expert_row) & (iota((n, n), 0) < iota((n, n), 1))
    rank = jnp.sum(same.astype(jnp.int32), axis=0, keepdims=True)
    target = (2 * expert_row + rank) * PIECES
    target_ref[...] = target
    slots = jnp.concatenate([target + k for k in range(PIECES)], axis=1)
    total = packed_ref.shape[0]
    placing = (iota((total, PIECES * n), 0) == slots).astype(F32).astype(BF16)
    gate = columns(gate_ref[...], n)
    gate = jnp.concatenate([gate] * (piece // n), axis=1)
    left = (gate * grad_ref[:, :piece].astype(F32)).astype(BF16)
    right = (gate * grad_ref[:, piece:].astype(F32)).astype(BF16)
    values = jnp.concatenate([tokens_ref[:, :piece], tokens_ref[:, piece:], left, right], axis=0)
    packed_ref[...] = dot(placing, values, (1, 0)).astype(BF16)


def prepare(tokens, routing, gate_prob, out_grad, slots):
    n, width = tokens.shape
    return pl.pallas_call(
        prep_body,
        out_shape=(
            pltpu.VMEM((slots * PIECES, width // 2), BF16),
            pltpu.VMEM((1, n), jnp.int32),
        ),
        compiler_params=pltpu.CompilerParams(vmem_limit_bytes=8 << 20),
        name="prep",
    )(*[far(v) for v in (tokens, routing.reshape(1, n), gate_prob.reshape(1, n), out_grad)])


def reorder_matrix(n, inverse):
    i, j = iota((n, n), 0), iota((n, n), 1)
    if inverse:
        i, j = j, i
    group = n // PIECES
    return (j == (i % group) * PIECES + i // group).astype(F32).astype(BF16)


def mid_body(
    recv_ref, up_hbm, down_hbm, up_far, down_far,
    back_hbm, rows_ref, hidden_hbm, pg_hbm, hidden_far, pg_far,
    up_own, down_own, back, hidden_own, pg_own, result, token_side, weight_sems, act_sems, back_sems,
):
    total, piece = recv_ref.shape
    width = 2 * piece
    chunk = 256
    group = chunk // PIECES

    fetches = (
        pltpu.make_async_copy(up_hbm, up_own, weight_sems.at[0]),
        pltpu.make_async_copy(down_hbm, down_own, weight_sems.at[1]),
    )
    for fetch in fetches:
        fetch.start()

    mix = reorder_matrix(chunk, False)
    for b in range(total // chunk):
        got = dot(mix, recv_ref[b * chunk : (b + 1) * chunk, :], (1, 0)).astype(BF16)
        for k in range(PIECES):
            rows_ref[b * group : (b + 1) * group, k * piece : (k + 1) * piece] = got[
                k * group : (k + 1) * group
            ]
    rows = rows_ref[:, :width]
    grads = rows_ref[:, width:]

    blocks = up_far.shape[1] // BLOCK
    parts = [slice(i * BLOCK, (i + 1) * BLOCK) for i in range(blocks)]
    jobs = [(part, up_far, down_far, hidden_far, pg_far) for part in parts]
    jobs += [(part, up_own, down_own, hidden_own, pg_own) for part in parts]
    stores = []

    def enter(job):
        part, up, down, _, _ = job
        return dot(rows, up[:, part], (1, 0)), dot(grads, down[part, :], (1, 1))

    def leave(k, v, hidden_grad):
        part, up, down, hidden_ref, pg_ref = jobs[k]
        sq = v * v
        t = jnp.tanh(v * (GELU_SLOPE + (GELU_SLOPE * GELU_CUBIC) * sq))
        p = 0.5 + 0.5 * t
        slope = p + v * (0.5 - 0.5 * (t * t)) * (GELU_SLOPE + (3 * GELU_SLOPE * GELU_CUBIC) * sq)
        hidden = (v * p).astype(BF16)
        pg = (hidden_grad * slope).astype(BF16)
        hidden_ref[:, part] = hidden
        pg_ref[:, part] = pg
        to_result = dot(hidden, down[part, :], (1, 0))
        to_token = dot(pg, up[:, part], (1, 1))
        if k == 0:
            result[...] = to_result
            token_side[...] = to_token
        else:
            result[...] += to_result
            token_side[...] += to_token
        if k >= blocks:
            for j, (near_ref, hbm_ref) in enumerate(((hidden_own, hidden_hbm), (pg_own, pg_hbm))):
                store = pltpu.make_async_copy(
                    near_ref.at[:, part], hbm_ref.at[:, part], act_sems.at[2 * (k - blocks) + j]
                )
                store.start()
                stores.append(store)

    pending = enter(jobs[0])
    for k in range(len(jobs)):
        if k + 1 == blocks:
            for fetch in fetches:
                fetch.wait()
        following = enter(jobs[k + 1]) if k + 1 < len(jobs) else None
        leave(k, *pending)
        pending = following

    mix = reorder_matrix(chunk, True)
    for b in range(total // chunk):
        part = slice(b * group, (b + 1) * group)
        stack = jnp.concatenate(
            [
                result[part, :piece],
                result[part, piece:],
                token_side[part, :piece],
                token_side[part, piece:],
            ],
            axis=0,
        ).astype(BF16)
        home = slice(b * chunk, (b + 1) * chunk)
        back[home, :] = dot(mix, stack, (1, 0)).astype(BF16)
        store = pltpu.make_async_copy(back.at[home, :], back_hbm.at[home, :], back_sems.at[b])
        store.start()
        stores.append(store)
    for store in stores:
        store.wait()


def expert_pass(received, up_own, down_own, up_far, down_far):
    total, piece = received.shape
    slots, width = total // PIECES, 2 * piece
    hidden = up_own.shape[1]
    vmem = pl.BlockSpec(memory_space=pltpu.VMEM)
    left = pl.BlockSpec(memory_space=pl.ANY)
    act = pltpu.VMEM((slots, hidden), BF16)
    act_hbm = pltpu.HBM((slots, hidden), BF16)
    blocks = hidden // BLOCK
    return pl.pallas_call(
        mid_body,
        in_specs=[vmem, left, left, vmem, vmem],
        out_specs=[left, vmem, left, left, vmem, vmem],
        out_shape=[
            pltpu.HBM((total, piece), BF16),
            pltpu.VMEM((slots, 2 * width), BF16),
            act_hbm, act_hbm, act, act,
        ],
        scratch_shapes=[
            pltpu.VMEM(up_own.shape, BF16),
            pltpu.VMEM(down_own.shape, BF16),
            pltpu.VMEM((total, piece), BF16),
            act, act,
            pltpu.VMEM((slots, width), F32),
            pltpu.VMEM((slots, width), F32),
            pltpu.SemaphoreType.DMA((2,)),
            pltpu.SemaphoreType.DMA((2 * blocks,)),
            pltpu.SemaphoreType.DMA((total // 256,)),
        ],
        compiler_params=pltpu.CompilerParams(vmem_limit_bytes=30 << 20),
        cost_estimate=pl.CostEstimate(
            flops=16 * slots * width * hidden,
            bytes_accessed=8 * width * hidden + 10 * slots * hidden,
            transcendentals=2 * slots * hidden,
        ),
        name="mid",
    )(near(received), far(up_own), far(down_own), near(up_far), near(down_far))


def collect_body(returned_ref, target_ref, gate_ref, grad_ref, output_ref, token_grad_ref, prob_ref):
    n, width = grad_ref.shape
    piece = width // 2
    total = returned_ref.shape[0]
    target = columns(target_ref[...], n)
    target = jnp.concatenate([target] * (total // n), axis=1)
    lane = iota((n, total), 1)
    picking = jnp.concatenate(
        [(lane == target + k).astype(F32).astype(BF16) for k in range(PIECES)], axis=0
    )
    got = dot(picking, returned_ref[...], (1, 0))
    gate = columns(gate_ref[...], n)
    gate = jnp.concatenate([gate] * (piece // n), axis=1)
    prob = jnp.zeros((n, 1), F32)
    for k in range(2):
        part = slice(k * piece, (k + 1) * piece)
        expert_tok = got[k * n : (k + 1) * n]
        output_ref[:, part] = (gate * expert_tok).astype(BF16)
        prob += jnp.sum(grad_ref[:, part].astype(F32) * expert_tok, axis=1, keepdims=True)
        token_grad_ref[:, part] = got[(2 + k) * n : (3 + k) * n].astype(BF16)
    prob_ref[...] = jnp.transpose(jnp.broadcast_to(prob, (n, n)))[:1]


def collect(returned, target, gate_prob, out_grad):
    n, width = out_grad.shape
    half = jax.ShapeDtypeStruct((n, width), BF16)
    output, token_grad, prob = pl.pallas_call(
        collect_body,
        out_shape=(half, half, jax.ShapeDtypeStruct((1, n), F32)),
        compiler_params=pltpu.CompilerParams(vmem_limit_bytes=8 << 20),
        name="collect",
    )(returned, target, gate_prob.reshape(1, n), out_grad)
    return output, token_grad, prob.reshape(n)


def local(tokens, routing, gate_prob, up_weight, down_weight, out_grad):
    token_count, width = tokens.shape
    experts = up_weight.shape[0] * lax.axis_size("ep")
    slots = 2 * experts

    def swap(value):
        return lax.ppermute(value, "dp", [(0, 1), (1, 0)])

    def exchange(value):
        value = value.reshape(experts, 2 * PIECES, width // 2)
        value = lax.all_to_all(value, "ep", 0, 0, tiled=True)
        return value.reshape(slots * PIECES, width // 2)

    up_own, down_own = up_weight[0], down_weight[0]
    packed, target = prepare(tokens, routing, gate_prob, out_grad, slots)
    up_far, down_far = swap(up_own), swap(down_own)
    received = exchange(packed)
    back, rows, hidden_own, pg_own, hidden_far, pg_far = expert_pass(
        received, up_own, down_own, up_far, down_far
    )
    returned = exchange(back)

    rows_all = jnp.concatenate([rows, swap(rows)], axis=0)
    hidden_all = jnp.concatenate([hidden_own, swap(hidden_far)], axis=0)
    pg_all = jnp.concatenate([pg_own, swap(pg_far)], axis=0)
    up_grad = dot(rows_all[:, :width], pg_all, (0, 0)).astype(BF16)[None]
    down_grad = dot(hidden_all, rows_all[:, width:], (0, 0)).astype(BF16)[None]

    output, token_grad, prob_grad = collect(returned, target, gate_prob, out_grad)
    return (output, token_grad, prob_grad, up_grad, down_grad)


def solution(mesh):
    rows = P(("ep", "dp"), None)
    flat = P(("ep", "dp"))
    up, down = P("ep", None, "dp"), P("ep", "dp", None)
    return jax.shard_map(
        local,
        mesh=mesh,
        in_specs=(rows, rows, flat, up, down, rows),
        out_specs=(rows, rows, flat, up, down),
        check_vma=False,
    )
```

time: 100 us -> 83.9 us (0.84)
  blocking collectives: 0 us -> 39.7 us
  waiting for transfers between devices: 41.3 us -> 17.5 us
  matrix products: 24.8 us -> 5.66 us
  starting transfers between devices: 23.6 us -> 8.58 us
  Pallas kernels: 0 us -> 10.3 us
  other arithmetic: 5.51 us -> 0 us
  local copies, waits for them, and re-layouts: 3.45 us -> 1.25 us
    all_to_all x0 -> x1, blocking collectives: none -> 39.7 us  [exchange(): value = lax.all_to_all(value, 'ep', 0, 0, tiled=True)]
    all_to_all x2 -> x1, waiting for transfers between devices: 38.6 us -> 17 us  [exchange(): value = lax.all_to_all(value, 'ep', 0, 0, tiled=True)]
    dot_general x12 -> x2, matrix products: 24.8 us -> 5.66 us  [dot(): lax.dot_general(a, b, ((dims[:1], dims[1:]), ((), ())), preferred_element...]
    all_to_all x2 -> x1, starting transfers between devices: 22.4 us -> 7.13 us  [exchange(): value = lax.all_to_all(value, 'ep', 0, 0, tiled=True)]
    pallas_call x0 -> x3, Pallas kernels: none -> 10.3 us  [the longest x1 6.99 us: expert_pass(): pl.pallas_call(mid_body, in_specs=[vmem, left, left, vmem, vmem], out_spe...]
    reduce_sum x2 -> x0, other arithmetic: 2.2 us -> none  [the longest x1 1.3 us: local(): prob_grad = jnp.sum(grad_wide * expert_tok, axis=1)]
    ppermute x5, waiting for transfers between devices: 2.7 us -> 0.53 us  [swap(): return lax.ppermute(value, 'dp', [(0, 1), (1, 0)])]
    reshape x3 -> x0, local copies, waits for them, and re-layouts: 1.77 us -> none  [the longest x1 1.18 us: exchange(): value = value.reshape(experts, capacity, 2 * width)]
  transfers between devices with their start and end apart: 7 -> 6, of which waited for: 4 -> 2; matrix products, arithmetic and copies ran while one was open for 15% -> 8% of each run, Pallas kernels for 0% -> 2%
where the time goes in v2:
time: 83.9 us; the launch traced here: 83.6 us
  blocking collectives  39.7 us (47%)
  waiting for transfers between devices  17.5 us (21%)
  Pallas kernels  10.3 us (12%)
  starting transfers between devices  8.58 us (10%)
  matrix products  5.66 us (7%)
  local copies, waits for them, and re-layouts  1.25 us (1%)
    all_to_all x1, blocking collectives, exchange(): value = lax.all_to_all(value, 'ep', 0, 0, tiled=True)  39.7 us
    all_to_all x1, waiting for transfers between devices, exchange(): value = lax.all_to_all(value, 'ep', 0, 0, tiled=True)  17 us
    all_to_all x1, starting transfers between devices, exchange(): value = lax.all_to_all(value, 'ep', 0, 0, tiled=True)  7.13 us
    pallas_call x1, Pallas kernels, expert_pass(): pl.pallas_call(mid_body, in_specs=[vmem, left, left, vmem, vmem], out_spe...  6.99 us
    dot_general x2, matrix products, dot(): lax.dot_general(a, b, ((dims[:1], dims[1:]), ((), ())), preferred_element...  5.66 us
    pallas_call x1, Pallas kernels, prepare(): pl.pallas_call(prep_body, out_shape=(pltpu.VMEM((slots * PIECES, width //...  1.84 us
  transfers between devices with their start and end apart: 6, of which 2 were waited for; matrix products, arithmetic and copies ran while one was open for 8% of the time, Pallas kernels for 2%

profile of v2, /device:TPU:32, one launch (start us, length us, event | category | flops | bytes accessed | tf_op | source)
XLA Modules:
  0.0 83.6 jit_solution(14036929425255089821)
XLA Ops:
  0.6 0.1 collective-permute-start
  0.7 0.5 collective-permute-start.1
  1.2 1.8 %prep.1 = (bf16[1024,384]{1,0:T(8,128)(2,1)S(1)}, s32[1,128]{1,0:T(1,128)S(1)}) custom-call(bf16[128,768]{1,0:T(8,128)(2,1)} %tokens_ref.1, s32[1,128]{1,0:T(1,128)} %bitcast.19, f32[1,128]{1,0:T(1,128)} %bitcast.16, bf16[128,768]{1,0:T(8,128)(2,1)} %grad_ref.3), custom_call_target="tpu_custom_call" | custom-call | tf_op jit(solution)/shard_map/prep/pallas_call | solution.py:60
  3.1 39.7 %all_to_all.10 = bf16[128,8,384]{2,1,0:T(8,128)(2,1)S(1)} all-to-all(bf16[128,8,384]{2,1,0:T(8,128)(2,1)S(1)} %bitcast.15), channel_id=1, replica_groups=mesh['ep'=128,'dp'=2] {'ep'}, dimensions={0} | all-to-all | bytes 1572864 | tf_op jit(solution)/shard_map/all_to_all | solution.py:256
  42.8 0.0 collective-permute-done.up_far
  42.8 0.0 collective-permute-done.1.down_far
  42.8 7.0 %mid.1 = (bf16[1024,384]{1,0:T(8,128)(2,1)}, bf16[256,1536]{1,0:T(8,128)(2,1)S(1)}, bf16[256,1536]{1,0:T(8,128)(2,1)}, bf16[256,1536]{1,0:T(8,128)(2,1)}, bf16[2...) custom-call(bf16[1024,384]{1,0:T(8,128)(2,1)S(1)} %bitcast.14, bf16[768,1536]{1,0:T(8,128)(2,1)} %bitcast.21, ...), custom_call_target="tpu_custom_call" | custom-call | flops 4831838208 | bytes 13369344 | tf_op jit(solution)/shard_map/mid/pallas_call | solution.py:181
  49.8 0.1 collective-permute-start.2
  49.9 7.1 %all-to-all-start.1 = ((bf16[128,8,384]{2,1,0:T(8,128)(2,1)}), bf16[128,8,384]{2,1,0:T(8,128)(2,1)S(1)}, u32[]{:S(2)}, u32[]{:S(2)}) async-start(bf16[128,8,384]{2,1,0:T(8,128)(2,1)} %bitcast.18), calls=%async_computation.1 | async-start | bytes 1572864 | tf_op jit(solution)/shard_map/all_to_all | solution.py:256
  57.0 0.3 collective-permute-start.3
  57.3 0.0 copy-start.2
  57.3 0.5 collective-permute-start.4
  57.8 0.1 constant_dynamic-update-slice_fusion.1
  57.8 0.0 collective-permute-done.2
  57.8 1.2 %constant_dynamic-update-slice_fusion = bf16[512,1536]{1,0:T(8,128)(2,1)S(1)} fusion(bf16[512,1536]{1,0:T(8,128)(2,1)S(1)} %constant_dynamic-update-slice_fusion.1, bf16[256,1536]{1,0:T(8,128)(2,1)} %collective-permute-done.2), kind=kLoop, calls=%fused_computation.12 | loop fusion | bytes 1572864 | tf_op jit(solution)/shard_map/concatenate | solution.py:268
  59.0 0.5 collective-permute-done.3
  59.6 0.0 copy-done.2
  59.6 2.8 %fusion = bf16[1,768,1536]{2,1,0:T(8,128)(2,1)} fusion(bf16[256,1536]{1,0:T(8,128)(2,1)S(1)} %collective-permute-done.3, bf16[256,1536]{1,0:T(8,128)(2,1)S(1)} %copy-done.2, bf16[512,1536]{1,0:T(8,128)(2,1)S(1)} %constant_dynamic-update-slice_fusion), kind=kOutput, calls=%fused_computation.2 | convolution fusion | flops 1212284928 | bytes 4718592 | tf_op jit(solution)/shard_map/dot_general | solution.py:20
  62.4 0.0 collective-permute-done.4
  62.4 0.0 copy-done.3
  62.4 2.8 %fusion.1 = bf16[1,1536,768]{2,1,0:T(8,128)(2,1)} fusion(bf16[256,1536]{1,0:T(8,128)(2,1)S(1)} %collective-permute-done.4, bf16[256,1536]{1,0:T(8,128)(2,1)S(1)} %copy-done.3, bf16[512,1536]{1,0:T(8,128)(2,1)S(1)} %constant_dynamic-update-slice_fusion), kind=kOutput, calls=%fused_computation.3 | convolution fusion | flops 1212284928 | bytes 4718592 | tf_op jit(solution)/shard_map/dot_general | solution.py:20
  65.2 17.0 %all-to-all-done.1 = bf16[128,8,384]{2,1,0:T(8,128)(2,1)S(1)} async-done(((bf16[128,8,384]{2,1,0:T(8,128)(2,1)}), bf16[128,8,384]{2,1,0:T(8,128)(2,1)S(1)}, u32[]{:S(2)}, u32[]{:S(2)}) %all-to-all-start.1) | async-done | bytes 786464 | tf_op jit(solution)/shard_map/all_to_all | solution.py:256
  82.2 0.0 copy-done
  82.2 1.4 %collect.1 = (bf16[128,768]{1,0:T(8,128)(2,1)}, bf16[128,768]{1,0:T(8,128)(2,1)}, f32[1,128]{1,0:T(1,128)}) custom-call(bf16[1024,384]{1,0:T(8,128)(2,1)S(1)} %bitcast.13, s32[1,128]{1,0:T(1,128)S(1)} %get-tuple-element.18.target_ref, f32[1,128]{1,0:T(1,128)S(1)} %bitcast.17, bf16[128,768]{1,0:T(8,128)(2,1)S(1)} %copy-done), custom_call_target="tpu_custom_call" | custom-call | tf_op jit(solution)/shard_map/collect/pallas_call | solution.py:237
  (4 shorter events, 0.0 us)
Async XLA Ops:
  0.6 42.1 %collective-permute-start = (bf16[768,1536]{1,0:T(8,128)(2,1)}, bf16[768,1536]{1,0:T(8,128)(2,1)S(1)}, u32[]{:S(2)}, u32[]{:S(2)}) collective-permute-start(bf16[768,1536]{1,0:T(8,128)(2,1)} %bitcast.20), channel_id=1, source_target_pairs={{0,1},{1,0},{2,3},{3,2},{4,5},{5,4},{6,7},{7,6},{8,9},{9,8},{10,11... | collective-permute-start | bytes 7077896 | tf_op jit(solution)/shard_map/ppermute | solution.py:252
  0.7 42.0 %collective-permute-start.1 = (bf16[1536,768]{1,0:T(8,128)(2,1)}, bf16[1536,768]{1,0:T(8,128)(2,1)S(1)}, u32[]{:S(2)}, u32[]{:S(2)}) collective-permute-start(bf16[1536,768]{1,0:T(8,128)(2,1)} %bitcast.22), channel_id=1, source_target_pairs={{0,1},{1,0},{2,3},{3,2},{4,5},{5,4},{6,7},{7,6},{8,9},{9,8},{10,11... | collective-permute-start | bytes 7077896 | tf_op jit(solution)/shard_map/ppermute | solution.py:252
  49.8 8.1 %collective-permute-start.2 = (bf16[256,1536]{1,0:T(8,128)(2,1)S(1)}, bf16[256,1536]{1,0:T(8,128)(2,1)}, u32[]{:S(2)}, u32[]{:S(2)}) collective-permute-start(bf16[256,1536]{1,0:T(8,128)(2,1)S(1)} %get-tuple-element.22), channel_id=1, source_target_pairs={{0,1},{1,0},{2,3},{3,2},{4,5},{5,4},{6,7},{7,6},{8,9},{9,8},{10,11... | collective-permute-start | bytes 2359304 | tf_op jit(solution)/shard_map/ppermute | solution.py:252
  49.9 32.3 %all-to-all-start.1 = ((bf16[128,8,384]{2,1,0:T(8,128)(2,1)}), bf16[128,8,384]{2,1,0:T(8,128)(2,1)S(1)}, u32[]{:S(2)}, u32[]{:S(2)}) async-start(bf16[128,8,384]{2,1,0:T(8,128)(2,1)} %bitcast.18), calls=%async_computation.1 | async-start | bytes 1572864 | tf_op jit(solution)/shard_map/all_to_all | solution.py:256
  57.0 2.6 %collective-permute-start.3 = (bf16[256,1536]{1,0:T(8,128)(2,1)S(1)}, bf16[256,1536]{1,0:T(8,128)(2,1)S(1)}, u32[]{:S(2)}, u32[]{:S(2)}) collective-permute-start(bf16[256,1536]{1,0:T(8,128)(2,1)S(1)} %get-tuple-element.24), channel_id=1, source_target_pairs={{0,1},{1,0},{2,3},{3,2},{4,5},{5,4},{6,7},{7,6},{8,9},{9,8},{10,11... | collective-permute-start | bytes 2359304 | tf_op jit(solution)/shard_map/ppermute | solution.py:252
  57.3 2.3 %copy-start.2 = (bf16[256,1536]{1,0:T(8,128)(2,1)S(1)}, bf16[256,1536]{1,0:T(8,128)(2,1)}, u32[]{:S(2)}) copy-start(bf16[256,1536]{1,0:T(8,128)(2,1)} %get-tuple-element.23) | copy-start | bytes 2359300
  57.3 5.1 %collective-permute-start.4 = (bf16[256,1536]{1,0:T(8,128)(2,1)S(1)}, bf16[256,1536]{1,0:T(8,128)(2,1)S(1)}, u32[]{:S(2)}, u32[]{:S(2)}) collective-permute-start(bf16[256,1536]{1,0:T(8,128)(2,1)S(1)} %get-tuple-element.26), channel_id=1, source_target_pairs={{0,1},{1,0},{2,3},{3,2},{4,5},{5,4},{6,7},{7,6},{8,9},{9,8},{10,11... | collective-permute-start | bytes 2359304 | tf_op jit(solution)/shard_map/ppermute | solution.py:252
  59.6 2.8 %copy-start.3 = (bf16[256,1536]{1,0:T(8,128)(2,1)S(1)}, bf16[256,1536]{1,0:T(8,128)(2,1)}, u32[]{:S(2)}) copy-start(bf16[256,1536]{1,0:T(8,128)(2,1)} %get-tuple-element.25) | copy-start | bytes 2359300
  62.4 19.8 %copy-start = (bf16[128,768]{1,0:T(8,128)(2,1)S(1)}, bf16[128,768]{1,0:T(8,128)(2,1)}, u32[]{:S(2)}) copy-start(bf16[128,768]{1,0:T(8,128)(2,1)} %grad_ref.3) | copy-start | bytes 589828
  62.4 19.8 %copy-start.1 = (f32[128]{0:T(128)S(1)}, f32[128]{0:T(128)}, u32[]{:S(2)}) copy-start(f32[128]{0:T(128)} %param.8) | copy-start | bytes 1540

commit v3 on v2

--- a/solution.py
+++ b/solution.py
@@ -76,9 +76,30 @@
     return (j == (i % group) * PIECES + i // group).astype(F32).astype(BF16)
 
 
+def reorder(recv_ref, rows_ref, top):
+    total, piece = recv_ref.shape
+    chunk = 256
+    group = chunk // PIECES
+    mix = reorder_matrix(chunk, False)
+    for b in range(total // chunk):
+        got = dot(mix, recv_ref[b * chunk : (b + 1) * chunk, :], (1, 0)).astype(BF16)
+        for k in range(PIECES):
+            rows_ref[top + b * group : top + (b + 1) * group, k * piece : (k + 1) * piece] = got[
+                k * group : (k + 1) * group
+            ]
+
+
+def activate(v, hidden_grad):
+    sq = v * v
+    t = jnp.tanh(v * (GELU_SLOPE + (GELU_SLOPE * GELU_CUBIC) * sq))
+    p = 0.5 + 0.5 * t
+    slope = p + v * (0.5 - 0.5 * (t * t)) * (GELU_SLOPE + (3 * GELU_SLOPE * GELU_CUBIC) * sq)
+    return (v * p).astype(BF16), (hidden_grad * slope).astype(BF16)
+
+
 def mid_body(
     recv_ref, up_hbm, down_hbm, up_far, down_far,
-    back_hbm, rows_ref, hidden_hbm, pg_hbm, hidden_far, pg_far,
+    back_hbm, rows_ref, hidden_hbm, pg_hbm,
     up_own, down_own, back, hidden_own, pg_own, result, token_side, weight_sems, act_sems, back_sems,
 ):
     total, piece = recv_ref.shape
@@ -93,36 +114,23 @@
     for fetch in fetches:
         fetch.start()
 
-    mix = reorder_matrix(chunk, False)
-    for b in range(total // chunk):
-        got = dot(mix, recv_ref[b * chunk : (b + 1) * chunk, :], (1, 0)).astype(BF16)
-        for k in range(PIECES):
-            rows_ref[b * group : (b + 1) * group, k * piece : (k + 1) * piece] = got[
-                k * group : (k + 1) * group
-            ]
+    reorder(recv_ref, rows_ref, 0)
     rows = rows_ref[:, :width]
     grads = rows_ref[:, width:]
 
     blocks = up_far.shape[1] // BLOCK
     parts = [slice(i * BLOCK, (i + 1) * BLOCK) for i in range(blocks)]
-    jobs = [(part, up_far, down_far, hidden_far, pg_far) for part in parts]
-    jobs += [(part, up_own, down_own, hidden_own, pg_own) for part in parts]
+    jobs = [(part, up_far, down_far) for part in parts]
+    jobs += [(part, up_own, down_own) for part in parts]
     stores = []
 
     def enter(job):
-        part, up, down, _, _ = job
+        part, up, down = job
         return dot(rows, up[:, part], (1, 0)), dot(grads, down[part, :], (1, 1))
 
     def leave(k, v, hidden_grad):
-        part, up, down, hidden_ref, pg_ref = jobs[k]
-        sq = v * v
-        t = jnp.tanh(v * (GELU_SLOPE + (GELU_SLOPE * GELU_CUBIC) * sq))
-        p = 0.5 + 0.5 * t
-        slope = p + v * (0.5 - 0.5 * (t * t)) * (GELU_SLOPE + (3 * GELU_SLOPE * GELU_CUBIC) * sq)
-        hidden = (v * p).astype(BF16)
-        pg = (hidden_grad * slope).astype(BF16)
-        hidden_ref[:, part] = hidden
-        pg_ref[:, part] = pg
+        part, up, down = jobs[k]
+        hidden, pg = activate(v, hidden_grad)
         to_result = dot(hidden, down[part, :], (1, 0))
         to_token = dot(pg, up[:, part], (1, 1))
         if k == 0:
@@ -132,6 +140,8 @@
             result[...] += to_result
             token_side[...] += to_token
         if k >= blocks:
+            hidden_own[:, part] = hidden
+            pg_own[:, part] = pg
             for j, (near_ref, hbm_ref) in enumerate(((hidden_own, hidden_hbm), (pg_own, pg_hbm))):
                 store = pltpu.make_async_copy(
                     near_ref.at[:, part], hbm_ref.at[:, part], act_sems.at[2 * (k - blocks) + j]
@@ -181,11 +191,11 @@
     return pl.pallas_call(
         mid_body,
         in_specs=[vmem, left, left, vmem, vmem],
-        out_specs=[left, vmem, left, left, vmem, vmem],
+        out_specs=[left, vmem, left, left],
         out_shape=[
             pltpu.HBM((total, piece), BF16),
             pltpu.VMEM((slots, 2 * width), BF16),
-            act_hbm, act_hbm, act, act,
+            act_hbm, act_hbm,
         ],
         scratch_shapes=[
             pltpu.VMEM(up_own.shape, BF16),
@@ -206,6 +216,57 @@
         ),
         name="mid",
     )(near(received), far(up_own), far(down_own), near(up_far), near(down_far))
+
+
+def weight_body(
+    far_ref, near_ref, up_ref, down_ref, hidden_ref, pg_ref, up_grad_ref, down_grad_ref, rows, turned
+):
+    slots, double = near_ref.shape
+    width = double // 2
+
+    @pl.when(pl.program_id(0) == 0)
+    def _():
+        rows[:slots, :] = near_ref[...]
+        reorder(far_ref, rows, slots)
+        turned[...] = jnp.transpose(rows[:, :width])
+
+    v = dot(rows[slots:, :width], up_ref[...], (1, 0))
+    hidden_grad = dot(rows[slots:, width:], down_ref[...], (1, 1))
+    hidden, pg = activate(v, hidden_grad)
+    hidden = jnp.concatenate([hidden_ref[...], hidden], axis=0)
+    pg = jnp.concatenate([pg_ref[...], pg], axis=0)
+    up_grad_ref[...] = dot(turned[...], pg, (1, 0)).astype(BF16)
+    down_grad_ref[...] = dot(hidden, rows[:, width:], (0, 0)).astype(BF16)
+
+
+def weight_gradients(received_far, rows, up, down, hidden, pg):
+    total, piece = received_far.shape
+    slots, double = rows.shape
+    width, units = up.shape
+    whole = lambda *shape: pl.BlockSpec(shape, lambda i: (0, 0))
+    wide = pl.BlockSpec((width, BLOCK), lambda i: (0, i))
+    tall = pl.BlockSpec((BLOCK, width), lambda i: (i, 0))
+    act = pl.BlockSpec((slots, BLOCK), lambda i: (0, i))
+    return pl.pallas_call(
+        weight_body,
+        grid=(units // BLOCK,),
+        in_specs=[whole(total, piece), whole(slots, double), wide, tall, act, act],
+        out_specs=[wide, tall],
+        out_shape=[
+            jax.ShapeDtypeStruct((width, units), BF16),
+            jax.ShapeDtypeStruct((units, width), BF16),
+        ],
+        scratch_shapes=[pltpu.VMEM((2 * slots, double), BF16), pltpu.VMEM((width, 2 * slots), BF16)],
+        compiler_params=pltpu.CompilerParams(
+            dimension_semantics=("arbitrary",), vmem_limit_bytes=20 << 20
+        ),
+        cost_estimate=pl.CostEstimate(
+            flops=12 * slots * width * units,
+            bytes_accessed=8 * width * units + 8 * slots * double,
+            transcendentals=slots * units,
+        ),
+        name="weights",
+    )(received_far, rows, *[far(v) for v in (up, down, hidden, pg)])
 
 
 def collect_body(returned_ref, target_ref, gate_ref, grad_ref, output_ref, token_grad_ref, prob_ref):
@@ -260,19 +321,12 @@
     packed, target = prepare(tokens, routing, gate_prob, out_grad, slots)
     up_far, down_far = swap(up_own), swap(down_own)
     received = exchange(packed)
-    back, rows, hidden_own, pg_own, hidden_far, pg_far = expert_pass(
-        received, up_own, down_own, up_far, down_far
-    )
+    received_far = swap(received)
+    back, rows, hidden, pg = expert_pass(received, up_own, down_own, up_far, down_far)
     returned = exchange(back)
-
-    rows_all = jnp.concatenate([rows, swap(rows)], axis=0)
-    hidden_all = jnp.concatenate([hidden_own, swap(hidden_far)], axis=0)
-    pg_all = jnp.concatenate([pg_own, swap(pg_far)], axis=0)
-    up_grad = dot(rows_all[:, :width], pg_all, (0, 0)).astype(BF16)[None]
-    down_grad = dot(hidden_all, rows_all[:, width:], (0, 0)).astype(BF16)[None]
-
+    up_grad, down_grad = weight_gradients(received_far, rows, up_own, down_own, hidden, pg)
     output, token_grad, prob_grad = collect(returned, target, gate_prob, out_grad)
-    return (output, token_grad, prob_grad, up_grad, down_grad)
+    return (output, token_grad, prob_grad, up_grad[None], down_grad[None])
 
 
 def solution(mesh):

time: 83.9 us -> 82.5 us (0.983)
  Pallas kernels: 10.3 us -> 19.2 us
  matrix products: 5.66 us -> 0 us
  waiting for transfers between devices: 17.5 us -> 14.8 us
  local copies, waits for them, and re-layouts: 1.25 us -> 0.01 us
    pallas_call x0 -> x1, Pallas kernels: none -> 9.12 us  [weight_gradients(): pl.pallas_call(weight_body, grid=(units // BLOCK,), in_specs=[whole(total...]
    dot_general x2 -> x0, matrix products: 5.66 us -> none  [dot(): lax.dot_general(a, b, ((dims[:1], dims[1:]), ((), ())), preferred_element...]
    all_to_all x1, waiting for transfers between devices: 17 us -> 12.5 us  [exchange(): value = lax.all_to_all(value, 'ep', 0, 0, tiled=True)]
    ppermute x5 -> x3, waiting for transfers between devices: 0.53 us -> 2.28 us  [swap(): return lax.ppermute(value, 'dp', [(0, 1), (1, 0)])]
    concatenate x1 -> x0, local copies, waits for them, and re-layouts: 1.19 us -> none  [local(): rows_all = jnp.concatenate([rows, swap(rows)], axis=0)]
  transfers between devices with their start and end apart: 6 -> 4, of which waited for: 2 -> 2; matrix products, arithmetic and copies ran while one was open for 8% -> 0% of each run, Pallas kernels for 2% -> 13%
where the time goes in v3:
time: 82.5 us; the launch traced here: 82.2 us
  blocking collectives  39.7 us (48%)
  Pallas kernels  19.2 us (23%)
  waiting for transfers between devices  14.8 us (18%)
  starting transfers between devices  7.81 us (9%)
    all_to_all x1, blocking collectives, exchange(): value = lax.all_to_all(value, 'ep', 0, 0, tiled=True)  39.7 us
    all_to_all x1, waiting for transfers between devices, exchange(): value = lax.all_to_all(value, 'ep', 0, 0, tiled=True)  12.5 us
    pallas_call x1, Pallas kernels, weight_gradients(): pl.pallas_call(weight_body, grid=(units // BLOCK,), in_specs=[whole(total...  9.12 us
    all_to_all x1, starting transfers between devices, exchange(): value = lax.all_to_all(value, 'ep', 0, 0, tiled=True)  7.13 us
    pallas_call x1, Pallas kernels, expert_pass(): pl.pallas_call(mid_body, in_specs=[vmem, left, left, vmem, vmem], out_spe...  6.85 us
    ppermute x3, waiting for transfers between devices, swap(): return lax.ppermute(value, 'dp', [(0, 1), (1, 0)])  2.28 us
    pallas_call x1, Pallas kernels, prepare(): pl.pallas_call(prep_body, out_shape=(pltpu.VMEM((slots * PIECES, width //...  1.84 us
  transfers between devices with their start and end apart: 4, of which 2 were waited for; matrix products, arithmetic and copies ran while one was open for 0% of the time, Pallas kernels for 13%

profile of v3, /device:TPU:32, one launch (start us, length us, event | category | flops | bytes accessed | tf_op | source)
XLA Modules:
  0.0 82.2 jit_solution(3802971367901822655)
XLA Ops:
  0.6 0.1 collective-permute-start
  0.7 0.5 collective-permute-start.1
  1.2 1.8 %prep.1 = (bf16[1024,384]{1,0:T(8,128)(2,1)S(1)}, s32[1,128]{1,0:T(1,128)S(1)}) custom-call(bf16[128,768]{1,0:T(8,128)(2,1)} %tokens_ref.1, s32[1,128]{1,0:T(1,128)} %bitcast.18, f32[1,128]{1,0:T(1,128)} %bitcast.15, bf16[128,768]{1,0:T(8,128)(2,1)} %grad_ref.3), custom_call_target="tpu_custom_call" | custom-call | tf_op jit(solution)/shard_map/prep/pallas_call | solution.py:60
  3.1 39.7 %all_to_all.10 = bf16[128,8,384]{2,1,0:T(8,128)(2,1)S(1)} all-to-all(bf16[128,8,384]{2,1,0:T(8,128)(2,1)S(1)} %bitcast.14), channel_id=1, replica_groups=mesh['ep'=128,'dp'=2] {'ep'}, dimensions={0} | all-to-all | bytes 1572864 | tf_op jit(solution)/shard_map/all_to_all | solution.py:317
  42.8 0.0 collective-permute-done.up_far
  42.8 0.0 collective-permute-done.1.down_far
  42.8 6.8 %mid.1 = (bf16[1024,384]{1,0:T(8,128)(2,1)}, bf16[256,1536]{1,0:T(8,128)(2,1)S(1)}, bf16[256,1536]{1,0:T(8,128)(2,1)}, bf16[256,1536]{1,0:T(8,128)(2,1)}) custom-call(bf16[1024,384]{1,0:T(8,128)(2,1)S(1)} %bitcast.12, bf16[768,1536]{1,0:T(8,128)(2,1)} %bitcast.20, bf16[1536,768]{1,0:T(8,128)(2,1)} %bitcast.23, ...), custom_call_target="tpu_custom_call" | custom-call | flops 4831838208 | bytes 13369344 | tf_op jit(solution)/shard_map/mid/pallas_call | solution.py:191
  49.6 7.1 %all-to-all-start.1 = ((bf16[128,8,384]{2,1,0:T(8,128)(2,1)}), bf16[128,8,384]{2,1,0:T(8,128)(2,1)S(1)}, u32[]{:S(2)}, u32[]{:S(2)}) async-start(bf16[128,8,384]{2,1,0:T(8,128)(2,1)} %bitcast.17), calls=%async_computation.1 | async-start | bytes 1572864 | tf_op jit(solution)/shard_map/all_to_all | solution.py:317
  56.8 0.1 collective-permute-start.2
  56.9 2.3 %collective-permute-done.2.far_ref = bf16[1024,384]{1,0:T(8,128)(2,1)S(1)} collective-permute-done((bf16[1024,384]{1,0:T(8,128)(2,1)S(1)}, bf16[1024,384]{1,0:T(8,128)(2,1)S(1)}, u32[]{:S(2)}, u32[]{:S(2)}) %collective-permute-start.2) | collective-permute-done | bytes 786464 | tf_op jit(solution)/shard_map/ppermute | solution.py:313
  59.1 0.0 copy-start
  59.1 0.0 copy-start.1
  59.1 9.1 %weights.1 = (bf16[768,1536]{1,0:T(8,128)(2,1)}, bf16[1536,768]{1,0:T(8,128)(2,1)}) custom-call(bf16[1024,384]{1,0:T(8,128)(2,1)S(1)} %collective-permute-done.2.far_ref, bf16[256,1536]{1,0:T(8,128)(2,1)S(1)} %get-tuple-element.22.near_ref, bf16[768,1536]{1,0:T(8,128)(2,1)} %bitcast.21, bf16[1536,768]{1,0:T(8,128)(2,1)} %bitcast.24, ...), custom_call_target="tpu_custom_call" | custom-call | flops 3623878656 | bytes 12582912 | tf_op jit(solution)/shard_map/weights/pallas_call | solution.py:250
  68.3 12.5 %all-to-all-done.1 = bf16[128,8,384]{2,1,0:T(8,128)(2,1)S(1)} async-done(((bf16[128,8,384]{2,1,0:T(8,128)(2,1)}), bf16[128,8,384]{2,1,0:T(8,128)(2,1)S(1)}, u32[]{:S(2)}, u32[]{:S(2)}) %all-to-all-start.1) | async-done | bytes 786464 | tf_op jit(solution)/shard_map/all_to_all | solution.py:317
  80.8 0.0 copy-done
  80.8 0.0 copy-done.1
  80.8 1.4 %collect.1 = (bf16[128,768]{1,0:T(8,128)(2,1)}, bf16[128,768]{1,0:T(8,128)(2,1)}, f32[1,128]{1,0:T(1,128)}) custom-call(bf16[1024,384]{1,0:T(8,128)(2,1)S(1)} %bitcast.11, s32[1,128]{1,0:T(1,128)S(1)} %get-tuple-element.18.target_ref, f32[1,128]{1,0:T(1,128)S(1)} %bitcast.16, bf16[128,768]{1,0:T(8,128)(2,1)S(1)} %copy-done), custom_call_target="tpu_custom_call" | custom-call | tf_op jit(solution)/shard_map/collect/pallas_call | solution.py:298
Async XLA Ops:
  0.6 42.1 %collective-permute-start = (bf16[768,1536]{1,0:T(8,128)(2,1)}, bf16[768,1536]{1,0:T(8,128)(2,1)S(1)}, u32[]{:S(2)}, u32[]{:S(2)}) collective-permute-start(bf16[768,1536]{1,0:T(8,128)(2,1)} %bitcast.19), channel_id=1, source_target_pairs={{0,1},{1,0},{2,3},{3,2},{4,5},{5,4},{6,7},{7,6},{8,9},{9,8},{10,11... | collective-permute-start | bytes 7077896 | tf_op jit(solution)/shard_map/ppermute | solution.py:313
  0.7 42.0 %collective-permute-start.1 = (bf16[1536,768]{1,0:T(8,128)(2,1)}, bf16[1536,768]{1,0:T(8,128)(2,1)S(1)}, u32[]{:S(2)}, u32[]{:S(2)}) collective-permute-start(bf16[1536,768]{1,0:T(8,128)(2,1)} %bitcast.22), channel_id=1, source_target_pairs={{0,1},{1,0},{2,3},{3,2},{4,5},{5,4},{6,7},{7,6},{8,9},{9,8},{10,11... | collective-permute-start | bytes 7077896 | tf_op jit(solution)/shard_map/ppermute | solution.py:313
  49.6 31.1 %all-to-all-start.1 = ((bf16[128,8,384]{2,1,0:T(8,128)(2,1)}), bf16[128,8,384]{2,1,0:T(8,128)(2,1)S(1)}, u32[]{:S(2)}, u32[]{:S(2)}) async-start(bf16[128,8,384]{2,1,0:T(8,128)(2,1)} %bitcast.17), calls=%async_computation.1 | async-start | bytes 1572864 | tf_op jit(solution)/shard_map/all_to_all | solution.py:317
  56.8 2.4 %collective-permute-start.2 = (bf16[1024,384]{1,0:T(8,128)(2,1)S(1)}, bf16[1024,384]{1,0:T(8,128)(2,1)S(1)}, u32[]{:S(2)}, u32[]{:S(2)}) collective-permute-start(bf16[1024,384]{1,0:T(8,128)(2,1)S(1)} %bitcast.13), channel_id=1, source_target_pairs={{0,1},{1,0},{2,3},{3,2},{4,5},{5,4},{6,7},{7,6},{8,9},{9,8},{10,11... | collective-permute-start | bytes 2359304 | tf_op jit(solution)/shard_map/ppermute | solution.py:313
  59.1 21.6 %copy-start = (bf16[128,768]{1,0:T(8,128)(2,1)S(1)}, bf16[128,768]{1,0:T(8,128)(2,1)}, u32[]{:S(2)}) copy-start(bf16[128,768]{1,0:T(8,128)(2,1)} %grad_ref.3) | copy-start | bytes 589828
  59.1 21.6 %copy-start.1 = (f32[128]{0:T(128)S(1)}, f32[128]{0:T(128)}, u32[]{:S(2)}) copy-start(f32[128]{0:T(128)} %param.8) | copy-start | bytes 1540

commit v4 on v3

--- a/solution.py
+++ b/solution.py
@@ -13,7 +13,21 @@
 GELU_SLOPE = math.sqrt(2.0 / math.pi)
 GELU_CUBIC = 0.044715
 PIECES = 4
+EP_X, EP_Z, EP_Y = 4, 8, 4
 BLOCK = 256
+
+
+def place_of(expert, core):
+    x, z, y = expert >> 5, (expert >> 2) & (EP_Z - 1), expert & (EP_Y - 1)
+    place = (z * EP_X + x) * EP_Y + y
+    return place + core * (EP_X * EP_Z * EP_Y - 1 - 2 * place)
+
+
+def participants():
+    walk = [
+        (x * EP_Z + z) * EP_Y + y for z in range(EP_Z) for x in range(EP_X) for y in range(EP_Y)
+    ]
+    return [[2 * e for e in walk], [2 * e + 1 for e in reversed(walk)]]
 
 
 def dot(a, b, dims):
@@ -42,7 +56,7 @@
     expert_row = routing_ref[...]
     same = (columns(expert_row, n) == expert_row) & (iota((n, n), 0) < iota((n, n), 1))
     rank = jnp.sum(same.astype(jnp.int32), axis=0, keepdims=True)
-    target = (2 * expert_row + rank) * PIECES
+    target = (2 * place_of(expert_row, lax.axis_index("dp")) + rank) * PIECES
     target_ref[...] = target
     slots = jnp.concatenate([target + k for k in range(PIECES)], axis=1)
     total = packed_ref.shape[0]
@@ -314,7 +328,9 @@
 
     def exchange(value):
         value = value.reshape(experts, 2 * PIECES, width // 2)
-        value = lax.all_to_all(value, "ep", 0, 0, tiled=True)
+        value = lax.all_to_all(
+            value, ("ep", "dp"), 0, 0, tiled=True, axis_index_groups=participants()
+        )
         return value.reshape(slots * PIECES, width // 2)
 
     up_own, down_own = up_weight[0], down_weight[0]

time: 82.5 us -> 79.1 us (0.959)
  waiting for transfers between devices: 14.8 us -> 11.2 us
  starting transfers between devices: 7.81 us -> 11.2 us
  blocking collectives: 39.7 us -> 36.4 us
    all_to_all x1, waiting for transfers between devices: 12.5 us -> 8.94 us  [exchange(): lax.all_to_all(value, ('ep', 'dp'), 0, 0, tiled=True, axis_index_groups=p...]
    all_to_all x1, starting transfers between devices: 7.13 us -> 10.5 us  [exchange(): lax.all_to_all(value, ('ep', 'dp'), 0, 0, tiled=True, axis_index_groups=p...]
    all_to_all x1, blocking collectives: 39.7 us -> 36.4 us  [exchange(): lax.all_to_all(value, ('ep', 'dp'), 0, 0, tiled=True, axis_index_groups=p...]
  transfers between devices with their start and end apart: 4 -> 4, of which waited for: 2 -> 2; matrix products, arithmetic and copies ran while one was open for 0% -> 0% of each run, Pallas kernels for 13% -> 14%
where the time goes in v4:
time: 79.1 us; the launch traced here: 78.7 us
  blocking collectives  36.4 us (46%)
  Pallas kernels  19.2 us (24%)
  starting transfers between devices  11.2 us (14%)
  waiting for transfers between devices  11.2 us (14%)
    all_to_all x1, blocking collectives, exchange(): lax.all_to_all(value, ('ep', 'dp'), 0, 0, tiled=True, axis_index_groups=p...  36.4 us
    all_to_all x1, starting transfers between devices, exchange(): lax.all_to_all(value, ('ep', 'dp'), 0, 0, tiled=True, axis_index_groups=p...  10.5 us
    pallas_call x1, Pallas kernels, weight_gradients(): pl.pallas_call(weight_body, grid=(units // BLOCK,), in_specs=[whole(total...  9.13 us
    all_to_all x1, waiting for transfers between devices, exchange(): lax.all_to_all(value, ('ep', 'dp'), 0, 0, tiled=True, axis_index_groups=p...  8.94 us
    pallas_call x1, Pallas kernels, expert_pass(): pl.pallas_call(mid_body, in_specs=[vmem, left, left, vmem, vmem], out_spe...  6.85 us
    ppermute x3, waiting for transfers between devices, swap(): return lax.ppermute(value, 'dp', [(0, 1), (1, 0)])  2.21 us
    pallas_call x1, Pallas kernels, prepare(): pl.pallas_call(prep_body, out_shape=(pltpu.VMEM((slots * PIECES, width //...  1.84 us
  transfers between devices with their start and end apart: 4, of which 2 were waited for; matrix products, arithmetic and copies ran while one was open for 0% of the time, Pallas kernels for 14%

profile of v4, /device:TPU:32, one launch (start us, length us, event | category | flops | bytes accessed | tf_op | source)
XLA Modules:
  0.0 78.7 jit_solution(5251269086972849835)
XLA Ops:
  0.6 0.1 collective-permute-start
  0.7 0.5 collective-permute-start.1
  1.2 1.8 %prep.1 = (bf16[1024,384]{1,0:T(8,128)(2,1)S(1)}, s32[1,128]{1,0:T(1,128)S(1)}) custom-call(bf16[128,768]{1,0:T(8,128)(2,1)} %tokens_ref.1, s32[1,128]{1,0:T(1,128)} %bitcast.18, f32[1,128]{1,0:T(1,128)} %bitcast.15, bf16[128,768]{1,0:T(8,128)(2,1)} %grad_ref.3), custom_call_target="tpu_custom_call" | custom-call | tf_op jit(solution)/shard_map/prep/pallas_call | solution.py:74
  3.1 36.4 %all_to_all.10 = bf16[128,8,384]{2,1,0:T(8,128)(2,1)S(1)} all-to-all(bf16[128,8,384]{2,1,0:T(8,128)(2,1)S(1)} %bitcast.14), channel_id=1, replica_groups={{0,2,4,6,64,66,68,70,128,130,132,134,192,194,196,198,8,10,12,14,72,74,7..., dimensions={0} | all-to-all | bytes 1572864 | tf_op jit(solution)/shard_map/all_to_all | solution.py:331
  39.5 0.0 collective-permute-done.up_far
  39.5 0.0 collective-permute-done.1.down_far
  39.5 6.8 %mid.1 = (bf16[1024,384]{1,0:T(8,128)(2,1)}, bf16[256,1536]{1,0:T(8,128)(2,1)S(1)}, bf16[256,1536]{1,0:T(8,128)(2,1)}, bf16[256,1536]{1,0:T(8,128)(2,1)}) custom-call(bf16[1024,384]{1,0:T(8,128)(2,1)S(1)} %bitcast.12, bf16[768,1536]{1,0:T(8,128)(2,1)} %bitcast.20, bf16[1536,768]{1,0:T(8,128)(2,1)} %bitcast.23, ...), custom_call_target="tpu_custom_call" | custom-call | flops 4831838208 | bytes 13369344 | tf_op jit(solution)/shard_map/mid/pallas_call | solution.py:205
  46.4 10.5 %all-to-all-start.1 = ((bf16[128,8,384]{2,1,0:T(8,128)(2,1)}), bf16[128,8,384]{2,1,0:T(8,128)(2,1)S(1)}, u32[]{:S(2)}, u32[]{:S(2)}) async-start(bf16[128,8,384]{2,1,0:T(8,128)(2,1)} %bitcast.17), calls=%async_computation.1 | async-start | bytes 1572864 | tf_op jit(solution)/shard_map/all_to_all | solution.py:331
  56.9 0.2 collective-permute-start.2
  57.0 2.2 %collective-permute-done.2.far_ref = bf16[1024,384]{1,0:T(8,128)(2,1)S(1)} collective-permute-done((bf16[1024,384]{1,0:T(8,128)(2,1)S(1)}, bf16[1024,384]{1,0:T(8,128)(2,1)S(1)}, u32[]{:S(2)}, u32[]{:S(2)}) %collective-permute-start.2) | collective-permute-done | bytes 786464 | tf_op jit(solution)/shard_map/ppermute | solution.py:327
  59.2 0.0 copy-start
  59.2 0.0 copy-start.1
  59.2 9.1 %weights.1 = (bf16[768,1536]{1,0:T(8,128)(2,1)}, bf16[1536,768]{1,0:T(8,128)(2,1)}) custom-call(bf16[1024,384]{1,0:T(8,128)(2,1)S(1)} %collective-permute-done.2.far_ref, bf16[256,1536]{1,0:T(8,128)(2,1)S(1)} %get-tuple-element.22.near_ref, bf16[768,1536]{1,0:T(8,128)(2,1)} %bitcast.21, bf16[1536,768]{1,0:T(8,128)(2,1)} %bitcast.24, ...), custom_call_target="tpu_custom_call" | custom-call | flops 3623878656 | bytes 12582912 | tf_op jit(solution)/shard_map/weights/pallas_call | solution.py:264
  68.4 8.9 %all-to-all-done.1 = bf16[128,8,384]{2,1,0:T(8,128)(2,1)S(1)} async-done(((bf16[128,8,384]{2,1,0:T(8,128)(2,1)}), bf16[128,8,384]{2,1,0:T(8,128)(2,1)S(1)}, u32[]{:S(2)}, u32[]{:S(2)}) %all-to-all-start.1) | async-done | bytes 786464 | tf_op jit(solution)/shard_map/all_to_all | solution.py:331
  77.3 0.0 copy-done
  77.3 0.0 copy-done.1
  77.3 1.4 %collect.1 = (bf16[128,768]{1,0:T(8,128)(2,1)}, bf16[128,768]{1,0:T(8,128)(2,1)}, f32[1,128]{1,0:T(1,128)}) custom-call(bf16[1024,384]{1,0:T(8,128)(2,1)S(1)} %bitcast.11, s32[1,128]{1,0:T(1,128)S(1)} %get-tuple-element.18.target_ref, f32[1,128]{1,0:T(1,128)S(1)} %bitcast.16, bf16[128,768]{1,0:T(8,128)(2,1)S(1)} %copy-done), custom_call_target="tpu_custom_call" | custom-call | tf_op jit(solution)/shard_map/collect/pallas_call | solution.py:312
Async XLA Ops:
  0.6 38.9 %collective-permute-start = (bf16[768,1536]{1,0:T(8,128)(2,1)}, bf16[768,1536]{1,0:T(8,128)(2,1)S(1)}, u32[]{:S(2)}, u32[]{:S(2)}) collective-permute-start(bf16[768,1536]{1,0:T(8,128)(2,1)} %bitcast.19), channel_id=1, source_target_pairs={{0,1},{1,0},{2,3},{3,2},{4,5},{5,4},{6,7},{7,6},{8,9},{9,8},{10,11... | collective-permute-start | bytes 7077896 | tf_op jit(solution)/shard_map/ppermute | solution.py:327
  0.7 38.8 %collective-permute-start.1 = (bf16[1536,768]{1,0:T(8,128)(2,1)}, bf16[1536,768]{1,0:T(8,128)(2,1)S(1)}, u32[]{:S(2)}, u32[]{:S(2)}) collective-permute-start(bf16[1536,768]{1,0:T(8,128)(2,1)} %bitcast.22), channel_id=1, source_target_pairs={{0,1},{1,0},{2,3},{3,2},{4,5},{5,4},{6,7},{7,6},{8,9},{9,8},{10,11... | collective-permute-start | bytes 7077896 | tf_op jit(solution)/shard_map/ppermute | solution.py:327
  46.4 30.9 %all-to-all-start.1 = ((bf16[128,8,384]{2,1,0:T(8,128)(2,1)}), bf16[128,8,384]{2,1,0:T(8,128)(2,1)S(1)}, u32[]{:S(2)}, u32[]{:S(2)}) async-start(bf16[128,8,384]{2,1,0:T(8,128)(2,1)} %bitcast.17), calls=%async_computation.1 | async-start | bytes 1572864 | tf_op jit(solution)/shard_map/all_to_all | solution.py:331
  56.9 2.4 %collective-permute-start.2 = (bf16[1024,384]{1,0:T(8,128)(2,1)S(1)}, bf16[1024,384]{1,0:T(8,128)(2,1)S(1)}, u32[]{:S(2)}, u32[]{:S(2)}) collective-permute-start(bf16[1024,384]{1,0:T(8,128)(2,1)S(1)} %bitcast.13), channel_id=1, source_target_pairs={{0,1},{1,0},{2,3},{3,2},{4,5},{5,4},{6,7},{7,6},{8,9},{9,8},{10,11... | collective-permute-start | bytes 2359304 | tf_op jit(solution)/shard_map/ppermute | solution.py:327
  59.2 18.1 %copy-start = (bf16[128,768]{1,0:T(8,128)(2,1)S(1)}, bf16[128,768]{1,0:T(8,128)(2,1)}, u32[]{:S(2)}) copy-start(bf16[128,768]{1,0:T(8,128)(2,1)} %grad_ref.3) | copy-start | bytes 589828
  59.2 18.1 %copy-start.1 = (f32[128]{0:T(128)S(1)}, f32[128]{0:T(128)}, u32[]{:S(2)}) copy-start(f32[128]{0:T(128)} %param.8) | copy-start | bytes 1540

commit v5 on v4

--- a/solution.py
+++ b/solution.py
@@ -19,13 +19,13 @@
 
 def place_of(expert, core):
     x, z, y = expert >> 5, (expert >> 2) & (EP_Z - 1), expert & (EP_Y - 1)
-    place = (z * EP_X + x) * EP_Y + y
+    place = (z * EP_Y + y) * EP_X + x
     return place + core * (EP_X * EP_Z * EP_Y - 1 - 2 * place)
 
 
 def participants():
     walk = [
-        (x * EP_Z + z) * EP_Y + y for z in range(EP_Z) for x in range(EP_X) for y in range(EP_Y)
+        (x * EP_Z + z) * EP_Y + y for z in range(EP_Z) for y in range(EP_Y) for x in range(EP_X)
     ]
     return [[2 * e for e in walk], [2 * e + 1 for e in reversed(walk)]]
 

time: 79.1 us -> 79.1 us (level)
  no operation moved by 1% of the time
where the time goes in v5:
time: 79.1 us; the launch traced here: 78.7 us
  blocking collectives  36.4 us (46%)
  Pallas kernels  19.2 us (24%)
  starting transfers between devices  11.2 us (14%)
  waiting for transfers between devices  11.2 us (14%)
    all_to_all x1, blocking collectives, exchange(): lax.all_to_all(value, ('ep', 'dp'), 0, 0, tiled=True, axis_index_groups=p...  36.4 us
    all_to_all x1, starting transfers between devices, exchange(): lax.all_to_all(value, ('ep', 'dp'), 0, 0, tiled=True, axis_index_groups=p...  10.5 us
    pallas_call x1, Pallas kernels, weight_gradients(): pl.pallas_call(weight_body, grid=(units // BLOCK,), in_specs=[whole(total...  9.12 us
    all_to_all x1, waiting for transfers between devices, exchange(): lax.all_to_all(value, ('ep', 'dp'), 0, 0, tiled=True, axis_index_groups=p...  8.95 us
    pallas_call x1, Pallas kernels, expert_pass(): pl.pallas_call(mid_body, in_specs=[vmem, left, left, vmem, vmem], out_spe...  6.85 us
    ppermute x3, waiting for transfers between devices, swap(): return lax.ppermute(value, 'dp', [(0, 1), (1, 0)])  2.21 us
    pallas_call x1, Pallas kernels, prepare(): pl.pallas_call(prep_body, out_shape=(pltpu.VMEM((slots * PIECES, width //...  1.84 us
  transfers between devices with their start and end apart: 4, of which 2 were waited for; matrix products, arithmetic and copies ran while one was open for 0% of the time, Pallas kernels for 14%

profile of v5, /device:TPU:32, one launch (start us, length us, event | category | flops | bytes accessed | tf_op | source)
XLA Modules:
  0.0 78.7 jit_solution(16918433866822333492)
XLA Ops:
  0.6 0.1 collective-permute-start
  0.7 0.5 collective-permute-start.1
  1.2 1.8 %prep.1 = (bf16[1024,384]{1,0:T(8,128)(2,1)S(1)}, s32[1,128]{1,0:T(1,128)S(1)}) custom-call(bf16[128,768]{1,0:T(8,128)(2,1)} %tokens_ref.1, s32[1,128]{1,0:T(1,128)} %bitcast.18, f32[1,128]{1,0:T(1,128)} %bitcast.15, bf16[128,768]{1,0:T(8,128)(2,1)} %grad_ref.3), custom_call_target="tpu_custom_call" | custom-call | tf_op jit(solution)/shard_map/prep/pallas_call | solution.py:74
  3.1 36.4 %all_to_all.10 = bf16[128,8,384]{2,1,0:T(8,128)(2,1)S(1)} all-to-all(bf16[128,8,384]{2,1,0:T(8,128)(2,1)S(1)} %bitcast.14), channel_id=1, replica_groups={{0,64,128,192,2,66,130,194,4,68,132,196,6,70,134,198,8,72,136,200,10,74..., dimensions={0} | all-to-all | bytes 1572864 | tf_op jit(solution)/shard_map/all_to_all | solution.py:331
  39.5 0.0 collective-permute-done.up_far
  39.5 0.0 collective-permute-done.1.down_far
  39.5 6.8 %mid.1 = (bf16[1024,384]{1,0:T(8,128)(2,1)}, bf16[256,1536]{1,0:T(8,128)(2,1)S(1)}, bf16[256,1536]{1,0:T(8,128)(2,1)}, bf16[256,1536]{1,0:T(8,128)(2,1)}) custom-call(bf16[1024,384]{1,0:T(8,128)(2,1)S(1)} %bitcast.12, bf16[768,1536]{1,0:T(8,128)(2,1)} %bitcast.20, bf16[1536,768]{1,0:T(8,128)(2,1)} %bitcast.23, ...), custom_call_target="tpu_custom_call" | custom-call | flops 4831838208 | bytes 13369344 | tf_op jit(solution)/shard_map/mid/pallas_call | solution.py:205
  46.4 10.5 %all-to-all-start.1 = ((bf16[128,8,384]{2,1,0:T(8,128)(2,1)}), bf16[128,8,384]{2,1,0:T(8,128)(2,1)S(1)}, u32[]{:S(2)}, u32[]{:S(2)}) async-start(bf16[128,8,384]{2,1,0:T(8,128)(2,1)} %bitcast.17), calls=%async_computation.1 | async-start | bytes 1572864 | tf_op jit(solution)/shard_map/all_to_all | solution.py:331
  56.9 0.2 collective-permute-start.2
  57.0 2.2 %collective-permute-done.2.far_ref = bf16[1024,384]{1,0:T(8,128)(2,1)S(1)} collective-permute-done((bf16[1024,384]{1,0:T(8,128)(2,1)S(1)}, bf16[1024,384]{1,0:T(8,128)(2,1)S(1)}, u32[]{:S(2)}, u32[]{:S(2)}) %collective-permute-start.2) | collective-permute-done | bytes 786464 | tf_op jit(solution)/shard_map/ppermute | solution.py:327
  59.2 0.0 copy-start
  59.2 0.0 copy-start.1
  59.2 9.1 %weights.1 = (bf16[768,1536]{1,0:T(8,128)(2,1)}, bf16[1536,768]{1,0:T(8,128)(2,1)}) custom-call(bf16[1024,384]{1,0:T(8,128)(2,1)S(1)} %collective-permute-done.2.far_ref, bf16[256,1536]{1,0:T(8,128)(2,1)S(1)} %get-tuple-element.22.near_ref, bf16[768,1536]{1,0:T(8,128)(2,1)} %bitcast.21, bf16[1536,768]{1,0:T(8,128)(2,1)} %bitcast.24, ...), custom_call_target="tpu_custom_call" | custom-call | flops 3623878656 | bytes 12582912 | tf_op jit(solution)/shard_map/weights/pallas_call | solution.py:264
  68.4 8.9 %all-to-all-done.1 = bf16[128,8,384]{2,1,0:T(8,128)(2,1)S(1)} async-done(((bf16[128,8,384]{2,1,0:T(8,128)(2,1)}), bf16[128,8,384]{2,1,0:T(8,128)(2,1)S(1)}, u32[]{:S(2)}, u32[]{:S(2)}) %all-to-all-start.1) | async-done | bytes 786464 | tf_op jit(solution)/shard_map/all_to_all | solution.py:331
  77.3 0.0 copy-done
  77.3 0.0 copy-done.1
  77.3 1.4 %collect.1 = (bf16[128,768]{1,0:T(8,128)(2,1)}, bf16[128,768]{1,0:T(8,128)(2,1)}, f32[1,128]{1,0:T(1,128)}) custom-call(bf16[1024,384]{1,0:T(8,128)(2,1)S(1)} %bitcast.11, s32[1,128]{1,0:T(1,128)S(1)} %get-tuple-element.18.target_ref, f32[1,128]{1,0:T(1,128)S(1)} %bitcast.16, bf16[128,768]{1,0:T(8,128)(2,1)S(1)} %copy-done), custom_call_target="tpu_custom_call" | custom-call | tf_op jit(solution)/shard_map/collect/pallas_call | solution.py:312
Async XLA Ops:
  0.6 38.9 %collective-permute-start = (bf16[768,1536]{1,0:T(8,128)(2,1)}, bf16[768,1536]{1,0:T(8,128)(2,1)S(1)}, u32[]{:S(2)}, u32[]{:S(2)}) collective-permute-start(bf16[768,1536]{1,0:T(8,128)(2,1)} %bitcast.19), channel_id=1, source_target_pairs={{0,1},{1,0},{2,3},{3,2},{4,5},{5,4},{6,7},{7,6},{8,9},{9,8},{10,11... | collective-permute-start | bytes 7077896 | tf_op jit(solution)/shard_map/ppermute | solution.py:327
  0.7 38.8 %collective-permute-start.1 = (bf16[1536,768]{1,0:T(8,128)(2,1)}, bf16[1536,768]{1,0:T(8,128)(2,1)S(1)}, u32[]{:S(2)}, u32[]{:S(2)}) collective-permute-start(bf16[1536,768]{1,0:T(8,128)(2,1)} %bitcast.22), channel_id=1, source_target_pairs={{0,1},{1,0},{2,3},{3,2},{4,5},{5,4},{6,7},{7,6},{8,9},{9,8},{10,11... | collective-permute-start | bytes 7077896 | tf_op jit(solution)/shard_map/ppermute | solution.py:327
  46.4 30.9 %all-to-all-start.1 = ((bf16[128,8,384]{2,1,0:T(8,128)(2,1)}), bf16[128,8,384]{2,1,0:T(8,128)(2,1)S(1)}, u32[]{:S(2)}, u32[]{:S(2)}) async-start(bf16[128,8,384]{2,1,0:T(8,128)(2,1)} %bitcast.17), calls=%async_computation.1 | async-start | bytes 1572864 | tf_op jit(solution)/shard_map/all_to_all | solution.py:331
  56.9 2.4 %collective-permute-start.2 = (bf16[1024,384]{1,0:T(8,128)(2,1)S(1)}, bf16[1024,384]{1,0:T(8,128)(2,1)S(1)}, u32[]{:S(2)}, u32[]{:S(2)}) collective-permute-start(bf16[1024,384]{1,0:T(8,128)(2,1)S(1)} %bitcast.13), channel_id=1, source_target_pairs={{0,1},{1,0},{2,3},{3,2},{4,5},{5,4},{6,7},{7,6},{8,9},{9,8},{10,11... | collective-permute-start | bytes 2359304 | tf_op jit(solution)/shard_map/ppermute | solution.py:327
  59.2 18.1 %copy-start = (bf16[128,768]{1,0:T(8,128)(2,1)S(1)}, bf16[128,768]{1,0:T(8,128)(2,1)}, u32[]{:S(2)}) copy-start(bf16[128,768]{1,0:T(8,128)(2,1)} %grad_ref.3) | copy-start | bytes 589828
  59.2 18.1 %copy-start.1 = (f32[128]{0:T(128)S(1)}, f32[128]{0:T(128)}, u32[]{:S(2)}) copy-start(f32[128]{0:T(128)} %param.8) | copy-start | bytes 1540
